TPU v7x, 512 devices: a whole 4x8x8 slice. The times are simulated.
512 devices in a mesh: row: 32 (over z, y_lo, core), col: 16 (over x, y_hi).
Axes of the slice: x: 4, y: 8 (y_hi: 4, y_lo: 2; y = y_hi * 2 + y_lo), z: 8, core: 2. Of those that a mesh axis runs over, the one named last changes fastest.
Arguments:
- pair_exchange: bfloat16 [1024, 16, 1024], P(('row', 'col')), may hold values from -6 to 6
- conduction: bfloat16 [1024, 4, 1024], P(('row', 'col')), may hold values from -6 to 6
- valence: bfloat16 [1024, 4, 1024], P(('row', 'col')), may hold values from -6 to 6
- coulomb: float32 [1024], replicated, may hold values from 0.5 to 5
- screening: float32 [289, 1024], replicated, may hold values from 0.1 to 1
- energies: float32 [1024, 16], P(('row', 'col')), may hold values from 1 to 9
- vectors: bfloat16 [1024, 512], P(('row', 'col')), may hold values from -6 to 6
- k_coords: int32 [1024, 2], P(('row', 'col')), may hold values from 0 to 31, as said below
Outputs:
- residual_block: float32 [1024, 512], P(('row', 'col'))
- alpha: float32 [32, 32], replicated
Inputs may be any that keep to these rules, and one draw needn't show every extreme that they name: `k_coords`: each row holds a k-point's coordinates on the periodic 32 x 32 mesh, first then second; every mesh point occurs exactly once.
All inputs are finite; a program needn't handle non-finite values.
Results may differ from a plain program's by a relative error of at most 0.0028.
Values may be sent and summed in bfloat16 or wider, within the bound.
A program may use at most 64 MiB of HBM per device.

v0:
```python
import functools

import jax
import jax.numpy as jnp
from jax import lax
from jax.sharding import Mesh
from jax.sharding import PartitionSpec as P

MX = 32
ROW = ("row_0", "row_1", "row_2")
COL = ("col_0", "col_1")
ROW_COL = ("row_0", "row_1", "row_2", "col_0", "col_1")


highest = lax.Precision.HIGHEST


def over_axes(x, axes):
    return functools.reduce(lax.psum, axes, x)


def pair_factors(conduction, valence):
    count, valence_count, plane_count = valence.shape
    joined = (
        valence.astype(jnp.float32)[:, :, None, :] * conduction.astype(jnp.float32)[:, None, :, :]
    )
    return joined.reshape(count, valence_count * conduction.shape[1], plane_count).astype(
        jnp.bfloat16
    )


def transfer_index(rows_at, cols_at, mesh_cols):
    delta_first = jnp.mod(rows_at[:, None, 0] - cols_at[None, :, 0], MX)
    delta_second = jnp.mod(rows_at[:, None, 1] - cols_at[None, :, 1], mesh_cols)
    fold_first = jnp.minimum(delta_first, MX - delta_first)
    fold_second = jnp.minimum(delta_second, mesh_cols - delta_second)
    return (fold_first * (mesh_cols // 2 + 1) + fold_second).astype(jnp.int32)


def on_device(pair_exchange, conduction, valence, coulomb, screening, energies, vectors, k_coords):
    local_count, band_count, plane_count = pair_exchange.shape
    vector_count = vectors.shape[1] // band_count
    row_count = lax.axis_size(ROW)
    col_count = lax.axis_size(COL)
    total_count = local_count * row_count * col_count
    mesh_cols = total_count // MX
    moving = vectors.reshape(local_count, band_count, vector_count)
    partial_density = jnp.einsum(
        "ktg,ktn->gn", pair_exchange, moving, preferred_element_type=jnp.float32
    )
    density = lax.psum(partial_density, ROW_COL)
    block_size = 128
    sweeps = plane_count // block_size
    col_cond, col_val, col_vec, col_at = (
        lax.all_gather(conduction, ROW, axis=0, tiled=True),
        lax.all_gather(valence, ROW, axis=0, tiled=True),
        lax.all_gather(vectors, ROW, axis=0, tiled=True),
        lax.all_gather(k_coords, ROW, axis=0, tiled=True),
    )
    row_cond, row_val, row_at = (
        lax.all_gather(conduction, COL, axis=0, tiled=True),
        lax.all_gather(valence, COL, axis=0, tiled=True),
        lax.all_gather(k_coords, COL, axis=0, tiled=True),
    )
    row_pairs = pair_factors(row_cond, row_val)
    col_pairs = pair_factors(col_cond, col_val)
    indices = transfer_index(row_at, col_at, mesh_cols)
    col_moving = col_vec.reshape(-1, band_count, vector_count)

    def square_sweep(sweep_index, running):
        anchor = sweep_index * block_size
        coupling = jnp.take(
            lax.dynamic_slice_in_dim(screening, anchor, block_size, 1), indices, axis=0
        )
        row_block = lax.dynamic_slice_in_dim(row_pairs, anchor, block_size, 2)
        col_block = lax.dynamic_slice_in_dim(col_pairs, anchor, block_size, 2)
        col_proj = jnp.einsum(
            "ktg,ktn->kng", col_block, col_moving, preferred_element_type=jnp.float32
        )
        potential = jnp.einsum("ijg,jng->ing", coupling, col_proj, precision=highest)
        return running + jnp.einsum(
            "ktg,kng->ktn", row_block.astype(jnp.float32), potential, precision=highest
        )

    forward = lax.fori_loop(
        0,
        sweeps,
        square_sweep,
        jnp.zeros((row_pairs.shape[0], band_count, vector_count), jnp.float32),
    )
    owned = lax.psum_scatter(
        forward.reshape(col_count, local_count, band_count, vector_count),
        COL,
        scatter_dimension=0,
        tiled=True,
    )[0]
    moving_wide = moving.astype(jnp.float32)
    exchange_term = jnp.einsum(
        "ktg,gn->ktn", pair_exchange.astype(jnp.float32) * coulomb, density, precision=highest
    )
    applied = (
        energies[:, :, None] * moving_wide
        + 2.0 / (total_count * band_count) * exchange_term
        - owned / total_count
    )
    gram = jnp.einsum("ktm,ktn->mn", moving_wide, applied, precision=highest)
    alpha = over_axes(gram, ROW_COL) / (total_count * band_count)
    residual = applied - jnp.einsum("ktm,mn->ktn", moving_wide, alpha, precision=highest)
    return (residual.reshape(local_count, band_count * vector_count), alpha)


def solution(mesh):
    split = Mesh(mesh.devices.reshape(8, 2, 2, 4, 4), ("row_0", "row_1", "row_2", "col_0", "col_1"))
    return jax.shard_map(
        on_device,
        mesh=split,
        in_specs=(
            P(ROW_COL, None, None),
            P(ROW_COL, None, None),
            P(ROW_COL, None, None),
            P(),
            P(),
            P(ROW_COL, None),
            P(ROW_COL, None),
            P(ROW_COL, None),
        ),
        out_specs=(P(ROW_COL, None), P()),
        check_vma=False,
    )
```

profile of v0, /device:TPU:1, one launch (start us, length us, event | category | flops | bytes accessed | tf_op | source)
XLA Modules:
  0.0 623.1 jit_solution(7728930901200443616)
XLA Ops:
  8.8 1.7 convolution_bitcast_fusion.1
  10.6 42.1 %all-gather.2 = s32[32,2,2]{2,1,0:T(2,128)S(1)} all-gather(s32[1,2,2]{2,1,0:T(2,128)} %bitcast.67), channel_id=1, replica_groups=mesh['row_0'=8,'row_1'=2,'row_2'=2,'col_0'=4,'col_1'=4] {'row_0','row_1'..., dimensions={0}, use_global_device_ids=true | all-gather | bytes 528 | tf_op jit(solution)/shard_map/all_gather | solution.py:58
  52.7 36.6 %all-gather.1 = s32[16,2,2]{2,1,0:T(2,128)S(1)} all-gather(s32[1,2,2]{2,1,0:T(2,128)} %bitcast.68), channel_id=1, replica_groups=mesh['row_0'=8,'row_1'=2,'row_2'=2,'col_0'=4,'col_1'=4] {'col_0','col_1'}, dimensions={0}, use_global_device_ids=true | all-gather | bytes 272 | tf_op jit(solution)/shard_map/all_gather | solution.py:63
  89.2 40.1 %all_gather.23 = bf16[64,4,1024]{2,1,0:T(4,128)(2,1)S(1)} all-gather(bf16[2,4,1024]{2,1,0:T(4,128)(2,1)} %param.12), channel_id=1, replica_groups=mesh['row_0'=8,'row_1'=2,'row_2'=2,'col_0'=4,'col_1'=4] {'row_0','row_1'..., dimensions={0}, use_global_device_ids=true | all-gather | bytes 540672 | tf_op jit(solution)/shard_map/all_gather | solution.py:56
  129.4 33.0 %all_gather.21 = bf16[32,4,1024]{2,1,0:T(4,128)(2,1)S(1)} all-gather(bf16[2,4,1024]{2,1,0:T(4,128)(2,1)} %param.12), channel_id=1, replica_groups=mesh['row_0'=8,'row_1'=2,'row_2'=2,'col_0'=4,'col_1'=4] {'col_0','col_1'}, dimensions={0}, use_global_device_ids=true | all-gather | bytes 278528 | tf_op jit(solution)/shard_map/all_gather | solution.py:62
  162.3 41.2 %all_gather.24 = bf16[64,4,1024]{2,1,0:T(4,128)(2,1)S(1)} all-gather(bf16[2,4,1024]{2,1,0:T(4,128)(2,1)} %param.11), channel_id=1, replica_groups=mesh['row_0'=8,'row_1'=2,'row_2'=2,'col_0'=4,'col_1'=4] {'row_0','row_1'..., dimensions={0}, use_global_device_ids=true | all-gather | bytes 540672 | tf_op jit(solution)/shard_map/all_gather | solution.py:55
  203.5 36.0 %all_gather.22 = bf16[32,4,1024]{2,1,0:T(4,128)(2,1)S(1)} all-gather(bf16[2,4,1024]{2,1,0:T(4,128)(2,1)} %param.11), channel_id=1, replica_groups=mesh['row_0'=8,'row_1'=2,'row_2'=2,'col_0'=4,'col_1'=4] {'col_0','col_1'}, dimensions={0}, use_global_device_ids=true | all-gather | bytes 278528 | tf_op jit(solution)/shard_map/all_gather | solution.py:61
  241.7 2.1 convert_element_type.42
  245.7 37.8 %all-gather = bf16[32,2,512]{2,1,0:T(2,128)(2,1)S(1)} all-gather(bf16[1,2,512]{2,1,0:T(2,128)(2,1)S(1)} %bitcast.66), channel_id=1, replica_groups=mesh['row_0'=8,'row_1'=2,'row_2'=2,'col_0'=4,'col_1'=4] {'row_0','row_1'..., dimensions={0}, use_global_device_ids=true | all-gather | bytes 67584 | tf_op jit(solution)/shard_map/all_gather | solution.py:57
  283.7 178.4 %while.14 = (s32[]{:T(128)}, f32[32,16,32]{2,1,0:T(8,128)S(1)}, bf16[32,16,1024]{2,1,0:T(8,128)(2,1)}, bf16[64,16,1024]{2,1,0:T(8,128)(2,1)}, bf16[64,16,32]{2,1...) while((s32[]{:T(128)}, f32[32,16,32]{2,1,0:T(8,128)S(1)}, ...), condition=%wide.region_2.3_spmd.clone, body=%wide.region_1.2_spmd.clone.sunk | while | flops 134656000 | bytes 12475081 | solution.py:85
  284.8 5.5 gather_fusion
  290.3 2.8 copy.37
  294.4 2.9 copy.36
  297.4 5.7 fusion.49
  307.1 5.5 gather_fusion
  312.6 2.8 copy.37
  316.7 2.9 copy.36
  319.7 5.7 fusion.49
  329.4 5.5 gather_fusion
  334.9 2.8 copy.37
  339.0 2.9 copy.36
  342.0 5.7 fusion.49
  351.7 5.5 gather_fusion
  357.2 2.8 copy.37
  361.3 2.9 copy.36
  364.3 5.7 fusion.49
  374.0 5.5 gather_fusion
  379.5 2.8 copy.37
  383.6 2.9 copy.36
  386.6 5.7 fusion.49
  396.3 5.5 gather_fusion
  401.8 2.8 copy.37
  405.9 2.9 copy.36
  408.9 5.7 fusion.49
  418.6 5.5 gather_fusion
  424.1 2.8 copy.37
  428.2 2.9 copy.36
  431.2 5.7 fusion.49
  440.9 5.5 gather_fusion
  446.4 2.8 copy.37
  450.5 2.9 copy.36
  453.5 5.7 fusion.49
  462.8 79.3 %reduce-scatter.2.cloned.1.call-done = f32[1,2,16,32]{3,2,1,0:T(8,128)} async-done(((f32[16,2,16,32]{3,2,1,0:T(8,128)}), f32[1,2,16,32]{3,2,1,0:T(8,128)}) %reduce-scatter.2.cloned.1.call-update) | async-done | bytes 4112 | tf_op jit(solution)/shard_map/reduce_scatter | solution.py:91
  543.4 23.6 %psum.43 = f32[32,32]{0,1:T(8,128)S(1)} all-reduce(f32[32,32]{0,1:T(8,128)S(1)} %convolution_bitcast_fusion.3), channel_id=1, replica_groups=mesh['row_0'=8,'row_1'=2,'row_2'=2,'col_0'=4,'col_1'=4] {'row_0'}, use_global_device_ids=true, to_apply=%region_4.5 | all-reduce | flops 1024 | bytes 8192 | tf_op jit(solution)/shard_map/psum | solution.py:19
  567.1 5.5 psum.44
  572.6 14.8 %psum.45 = f32[32,32]{0,1:T(8,128)S(1)} all-reduce(f32[32,32]{0,1:T(8,128)S(1)} %psum.44), channel_id=1, replica_groups=mesh['row_0'=8,'row_1'=2,'row_2'=2,'col_0'=4,'col_1'=4] {'row_2'}, use_global_device_ids=true, to_apply=%region_6.7 | all-reduce | flops 1024 | bytes 8192 | tf_op jit(solution)/shard_map/psum | solution.py:19
  587.4 12.2 %psum.46 = f32[32,32]{0,1:T(8,128)S(1)} all-reduce(f32[32,32]{0,1:T(8,128)S(1)} %psum.45), channel_id=1, replica_groups=mesh['row_0'=8,'row_1'=2,'row_2'=2,'col_0'=4,'col_1'=4] {'col_0'}, use_global_device_ids=true, to_apply=%region_7.8 | all-reduce | flops 1024 | bytes 8192 | tf_op jit(solution)/shard_map/psum | solution.py:19
  599.6 14.6 %psum.47 = f32[32,32]{0,1:T(8,128)S(1)} all-reduce(f32[32,32]{0,1:T(8,128)S(1)} %psum.46), channel_id=1, replica_groups=mesh['row_0'=8,'row_1'=2,'row_2'=2,'col_0'=4,'col_1'=4] {'col_1'}, use_global_device_ids=true, to_apply=%region_8.9 | all-reduce | flops 1024 | bytes 8192 | tf_op jit(solution)/shard_map/psum | solution.py:19
  (101 shorter events, 51.5 us)
Async XLA Ops:
  8.0 454.8 %all-reduce.2.cloned.1.call-start = ((), (), s32[]{:S(2)}) async-start(), calls=%async_computation.1 | async-start | bytes 262144 | tf_op jit(solution)/shard_map/psum | solution.py:51
  10.5 531.6 %reduce-scatter.2.cloned.1.call-start = ((), (), s32[]{:S(2)}) async-start(), calls=%async_computation.2 | async-start | bytes 278528 | tf_op jit(solution)/shard_map/reduce_scatter | solution.py:91
  243.9 1.7 copy-start.2
  283.6 258.5 %copy-start.1 = (bf16[2,16,1024]{2,1,0:T(8,128)(2,1)S(1)}, bf16[2,16,1024]{2,1,0:T(8,128)(2,1)}, u32[]{:S(2)}) copy-start(bf16[2,16,1024]{2,1,0:T(8,128)(2,1)} %param.10) | copy-start | bytes 196612
  283.6 258.5 %copy-start.3 = (f32[1024]{0:T(1024)S(1)}, f32[1024]{0:T(1024)}, u32[]{:S(2)}) copy-start(f32[1024]{0:T(1024)} %param.13) | copy-start | bytes 12292
  283.6 258.4 %copy-start.4 = (f32[2,16]{1,0:T(2,128)S(1)}, f32[2,16]{1,0:T(2,128)}, u32[]{:S(2)}) copy-start(f32[2,16]{1,0:T(2,128)} %param.15) | copy-start | bytes 388
  462.1 0.7 copy-start
Sparse Core Ops, SparseCore 0:
  13.8 271.8 all-reduce.1
Sparse Core Ops, SparseCore 1:
  462.9 79.1 reduce-scatter.1
where the time goes:
time: 630 us; the launch traced here: 623 us
  blocking collectives  337 us (53%)
  local copies, waits for them, and re-layouts  115 us (18%)
  waiting for transfers between devices  79.3 us (13%)
  matrix products  70.7 us (11%)
  between operations  15.6 us (2%)
    reduce_scatter x1, waiting for transfers between devices, on_device(): lax.psum_scatter(forward.reshape(col_count, local_count, band_count, vect...  79.3 us
    psum x5, blocking collectives, over_axes(): return functools.reduce(lax.psum, axes, x)  70.7 us
    gather x16, local copies, waits for them, and re-layouts, square_sweep(): jnp.take(lax.dynamic_slice_in_dim(screening, anchor, block_size, 1), indi...  66.3 us
    dot_general x8, matrix products, square_sweep(): jnp.einsum('ijg,jng->ing', coupling, col_proj, precision=highest)  45.6 us
    all_gather x1, blocking collectives, on_device(): lax.all_gather(k_coords, ROW, axis=0, tiled=True)  42.1 us
    all_gather x1, blocking collectives, on_device(): lax.all_gather(conduction, ROW, axis=0, tiled=True)  41.2 us
    all_gather x1, blocking collectives, on_device(): lax.all_gather(valence, ROW, axis=0, tiled=True)  40.1 us
    all_gather x1, blocking collectives, on_device(): lax.all_gather(vectors, ROW, axis=0, tiled=True)  37.8 us
  transfers between devices with their start and end apart: 2, of which 1 were waited for; matrix products, arithmetic and copies ran while one was open for 30% of the time, Pallas kernels for 0%

commit v1 on v0

v1 whole, which is shorter than its diff:
```python
import jax
import jax.numpy as jnp
import numpy as np
from jax import lax
from jax.experimental import pallas as pl
from jax.experimental.pallas import tpu as pltpu
from jax.sharding import PartitionSpec as P

MESH = pl.DeviceIdType.MESH
HIGH = lax.Precision.HIGHEST
F32 = jnp.float32
BF16 = jnp.bfloat16

NR, NC = 32, 16
NK, NT = 1024, 16384
NQ = 289
QPAD = 384
X_COORD_ROW, X_COORD_COL, X_PROJ_ROW, X_PROJ_COL, X_DENS_ROW, X_DENS_COL, X_DENS_OUT = range(7)
X_POT_COL, X_POT_ROW, X_ALPHA_COL, X_ALPHA_ROW = range(7, 11)


def real_basis():
    points = np.arange(32)[None, :]
    order = np.arange(32)[:, None]
    freq = np.where(order <= 16, order, order - 16)
    angle = 2 * np.pi * freq * points / 32
    basis = np.where(order <= 16, np.cos(angle), np.sin(angle)) * np.sqrt(2 / 32)
    basis[[0, 16]] *= np.sqrt(0.5)
    return basis, freq[:, 0]


def two_parts(table):
    high = table.astype(BF16)
    return high, (table - high.astype(np.float64)).astype(BF16)


def tables():
    basis, freq = real_basis()
    fold = np.arange(17)
    weight = np.where((fold == 0) | (fold == 16), 1.0, 2.0)
    cosine = weight[None, :] * np.cos(2 * np.pi * freq[:, None] * fold[None, :] / 32)
    modes = np.zeros((NK, QPAD))
    modes[:, :NQ] = np.kron(cosine, cosine)
    return np.concatenate(two_parts(basis), axis=1), *two_parts(modes)


def iota(shape, dim):
    return lax.broadcasted_iota(jnp.int32, shape, dim)


def one_hot(mask):
    return jnp.where(mask, 1.0, 0.0).astype(F32)


def dot(a, b, ca=1, cb=0, precision=None):
    return lax.dot_general(
        a, b, (((ca,), (cb,)), ((), ())), precision=precision, preferred_element_type=F32
    )


def split(v):
    high = v.astype(BF16)
    return high, (v - high.astype(F32)).astype(BF16)


def fold(v, *shifts):
    for shift in shifts:
        v = v + pltpu.roll(v, shift, 1)
    return v


def kernel(
    pe_ref, cond_ref, val_ref, coul_ref, en_ref, vec_ref, kc_ref, q2_ref, scr_hbm, mhi_hbm, mlo_hbm,
    out_ref, alpha_ref,
    v8, pairs, lk, pk, coulexp, c8,
    p_out, p_in, q_out, q_in, d_out, d_in, e_out, e_in, f_out, f_in,
    k_out, k_in, h_out, h_in, c16,
    z_out, z_in, y_out, y_in, a_out, a_in, b_out, b_in,
    arow, brow, tt_hi, tt_lo, lam, wt, perm_f, perm_b, scr, m_hi, m_lo,
    send_sems, recv_sems, local_sems,
):
    r, c = lax.axis_index("row"), lax.axis_index("col")
    sizes = {"row": (NR, r), "col": (NC, c)}

    def peers(axis, body):
        size, me = sizes[axis]
        half = size // 2

        def step(i, carry):
            ahead = jnp.where(i < half, half + i, i - half + 1)
            body(lax.rem(me + ahead, size))
            return carry

        lax.fori_loop(0, size - 1, step, 0)

    def send(axis, which, source, target):
        me = sizes[axis][1]

        def one(peer):
            pltpu.make_async_remote_copy(
                src_ref=source(peer),
                dst_ref=target.at[me],
                send_sem=send_sems.at[which],
                recv_sem=recv_sems.at[which],
                device_id={axis: peer},
                device_id_type=MESH,
            ).start()

        peers(axis, one)

    def wait_all(axis, sems, which, target):
        many = target.at[pl.ds(0, sizes[axis][0] - 1)]
        pltpu.make_async_copy(many, many, sems.at[which]).wait()

    def arrived(axis, which, target):
        wait_all(axis, recv_sems, which, target)

    barrier = pltpu.get_barrier_semaphore()
    for axis in ("row", "col"):
        peers(
            axis,
            lambda peer, axis=axis: pl.semaphore_signal(
                barrier, inc=1, device_id={axis: peer}, device_id_type=MESH
            ),
        )
    near = pl.multiple_of((r // 8) * 128, 128)
    far = pl.multiple_of((r // 8) * 128 + 512, 128)
    fetches = [
        pltpu.make_async_copy(
            scr_hbm.at[:, pl.ds(near, 128)], scr.at[0, pl.ds(0, NQ), :], local_sems.at[0]
        ),
        pltpu.make_async_copy(
            scr_hbm.at[:, pl.ds(far, 128)], scr.at[1, pl.ds(0, NQ), :], local_sems.at[1]
        ),
        pltpu.make_async_copy(mhi_hbm, m_hi, local_sems.at[2]),
        pltpu.make_async_copy(mlo_hbm, m_lo, local_sems.at[3]),
    ]
    for fetch in fetches:
        fetch.start()

    place = iota((1, 128), 1) - 4 * r
    k_row = jnp.zeros((1, 128), jnp.int32)
    for q in range(4):
        k_row = jnp.where(place == q, kc_ref[q // 2, q % 2], k_row)
    k_out[...] = k_row.astype(F32)

    vec = vec_ref[...].astype(F32)
    for i in range(8):
        v8[i : i + 1, :] = vec[i // 4 : i // 4 + 1, (i % 4) * 128 : (i % 4 + 1) * 128]
    row32, lane32 = iota((32, 128), 0), iota((32, 128), 1)
    lane_is_t = (row32 & 3) == (lane32 >> 5)
    spread = one_hot((iota((32, 8), 0) >> 2) == iota((32, 8), 1))
    gather8 = one_hot((iota((8, 32), 1) >> 2) == iota((8, 32), 0))
    wide = dot(spread.astype(BF16), v8[...].astype(BF16))
    x128 = fold(jnp.where(lane_is_t, wide, 0.0), 64, 32)

    for k in range(2):
        cond = cond_ref[k].astype(F32)
        val = val_ref[k].astype(F32)
        for v in range(4):
            at = 16 * k + 4 * v
            pairs[at : at + 4, :] = val[v : v + 1, :] * cond
    pair_rows = pairs[...].astype(BF16)
    lk[0:32, :] = pair_rows[:, :512]
    lk[32:64, :] = pair_rows[:, 512:]
    row64, lane64 = iota((64, 128), 0), iota((64, 128), 1)
    own64 = ((row64 >> 5) == ((lane64 >> 5) & 1)) & (((row64 >> 4) & 1) == (lane64 >> 6))
    x_block = jnp.where(own64, jnp.concatenate([x128, x128], axis=0), 0.0).astype(BF16)
    p_out[...] = dot(lk[...], x_block, 0, 0).astype(BF16).reshape(NR, NC, 128)

    for k in range(2):
        for j in range(4):
            at = 32 * j + 16 * k
            pk[at : at + 16, :] = pe_ref[k, :, j * 256 : (j + 1) * 256]
    own128 = (iota((128, 128), 0) >> 5) == (iota((128, 128), 1) >> 5)
    x_quarter = jnp.where(own128, jnp.concatenate([x128] * 4, axis=0), 0.0).astype(BF16)
    d_out[...] = dot(pk[...], x_quarter, 0, 0).reshape(NR, 8, 128)

    pl.semaphore_wait(barrier, NR + NC - 2)
    send("row", X_COORD_ROW, lambda peer: k_out, k_in)
    send("row", X_PROJ_ROW, lambda peer: p_out.at[peer], p_in)
    send("row", X_DENS_ROW, lambda peer: d_out.at[peer], d_in)
    k_in[pl.ds(r, 1)] = k_out[...].reshape(1, 1, 128)
    p_in[pl.ds(r, 1)] = p_out[pl.ds(r, 1)]
    d_in[pl.ds(r, 1)] = d_out[pl.ds(r, 1)]

    def build_perm(i, carry):
        at = pl.multiple_of(i * 128, 128)
        row, col = iota((128, 512), 0) + i * 128, iota((128, 512), 1)
        perm_f[pl.ds(at, 128), :] = one_hot(col == ((row & 31) << 4) + (row >> 5)).astype(BF16)
        perm_b[pl.ds(at, 128), :] = one_hot(col == ((row & 15) << 5) + (row >> 4)).astype(BF16)
        return carry

    lax.fori_loop(0, 4, build_perm, 0)
    c8[...] = jnp.zeros((8, 256), F32)
    for j in range(4):
        c8[j : j + 1, :] = coul_ref[:, j * 256 : (j + 1) * 256]
    expand8 = one_hot(iota((8, 128), 0) == (iota((8, 128), 1) >> 5))
    coulexp[...] = dot(c8[...], expand8, 0, 0, precision=HIGH)

    energy = jnp.concatenate(
        [jnp.broadcast_to(en_ref[k : k + 1, :], (16, 16)) for k in range(2)], axis=0
    )
    same = (iota((32, 16), 0) & 15) == iota((32, 16), 1)
    e_col = jnp.sum(jnp.where(same, energy, 0.0), axis=1, keepdims=True)
    ex128 = e_col * x128
    alpha_energy = dot(x128, ex128, 0, 0, precision=HIGH)[:32]

    arrived("row", X_COORD_ROW, k_in)
    h_out[...] = jnp.sum(k_in[...], axis=0)
    send("col", X_COORD_COL, lambda peer: h_out, h_in)
    h_in[pl.ds(c, 1)] = h_out[...].reshape(1, 1, 128)

    for fetch in fetches:
        fetch.wait()
    chosen = (r % 8) * 16 + c
    seen = (iota((QPAD, 128), 0) < NQ) & (iota((QPAD, 128), 1) == chosen)
    columns = [jnp.sum(jnp.where(seen, scr[h], 0.0), axis=1, keepdims=True) for h in range(2)]
    lane_q = iota((QPAD, 128), 1)
    s_hi, s_lo = split(jnp.where(((lane_q >> 5) & 1) == 0, columns[0], columns[1]))

    def build_lam(i, carry):
        at = pl.multiple_of(i * 256, 256)
        high, low = m_hi[pl.ds(at, 256), :], m_lo[pl.ds(at, 256), :]
        lam[pl.ds(at, 256), :] = dot(high, s_hi) + dot(high, s_lo) + dot(low, s_hi)
        return carry

    lax.fori_loop(0, 4, build_lam, 0)

    arrived("row", X_PROJ_ROW, p_in)
    mixed = dot(perm_f[...], p_in[...].reshape(512, 128)).astype(BF16)
    q_out[...] = mixed.reshape(NC, NR, 128)
    send("col", X_PROJ_COL, lambda peer: q_out.at[peer], q_in)
    q_in[pl.ds(c, 1)] = q_out[pl.ds(c, 1)]
    arrived("row", X_DENS_ROW, d_in)
    e_out[...] = jnp.sum(d_in[...], axis=0)
    send("col", X_DENS_COL, lambda peer: e_out, e_in)
    e_in[pl.ds(c, 1)] = e_out[...].reshape(1, 8, 128)

    arrived("col", X_COORD_COL, h_in)
    for i in range(NC):
        c16[i : i + 1, :] = h_in[i]
    repeat = one_hot(iota((16, 512), 0) == (iota((16, 512), 1) >> 5)).astype(BF16)
    spread_c = dot(c16[...].astype(BF16), repeat, 0, 0)
    row128, lane512 = iota((128, 512), 0), iota((128, 512), 1)
    kept = jnp.where((row128 >> 2) == (lane512 & 31), spread_c, 0.0).astype(BF16)
    pick = one_hot((iota((128, 128), 0) >> 5) == (iota((128, 128), 1) & 3)).astype(BF16)
    coords = dot(pick, kept)
    hot = one_hot(coords == (row128 & 31).astype(F32)).astype(BF16)
    q2 = q2_ref[...]
    for k in range(2):
        at = 64 * k
        first, second = hot[at : at + 32], hot[at + 32 : at + 64]
        arow[k] = dot(q2, jnp.concatenate([first, first], axis=0))
        brow[k] = dot(q2, jnp.concatenate([second, second], axis=0))

    def build_basis(j, carry):
        at = pl.multiple_of(j * 32, 32)
        for k in range(2):
            high, low = split(arow[k, pl.ds(j, 1), :] * brow[k])
            tt_hi[k, pl.ds(at, 32), :] = high
            tt_lo[k, pl.ds(at, 32), :] = low
        return carry

    lax.fori_loop(0, 32, build_basis, 0)

    arrived("col", X_PROJ_COL, q_in)
    proj = q_in[...].reshape(512, 128)
    lane256 = iota((256, 128), 1)

    def one_block(i, total):
        at = pl.multiple_of(i * 256, 256)
        parts = [
            dot(tt_hi[k, pl.ds(at, 256), :], proj) + dot(tt_lo[k, pl.ds(at, 256), :], proj)
            for k in range(2)
        ]
        mode = fold(jnp.where(lane256 < 64, parts[0], parts[1]), 64)
        scaled = lam[pl.ds(at, 256), :] * mode
        high, low = split(jnp.transpose(scaled)[:64])
        wt[0:64, pl.ds(at, 256)] = high
        wt[64:128, pl.ds(at, 256)] = low
        return total + dot(mode.astype(BF16), scaled.astype(BF16), 0, 0)

    alpha_direct = lax.fori_loop(0, 4, one_block, jnp.zeros((128, 128), F32))
    for k in range(2):
        both = dot(wt[...], tt_hi[k])
        back = both[:64] + both[64:] + dot(wt[0:64, :], tt_lo[k])
        coords_free = jnp.transpose(back)
        brow_at = 64 * k
        lam[0:512, brow_at : brow_at + 64] = coords_free
    z_out[...] = lam[0:512, :].astype(BF16).reshape(NC, NR, 128)
    send("col", X_POT_COL, lambda peer: z_out.at[peer], z_in)
    z_in[pl.ds(c, 1)] = z_out[pl.ds(c, 1)]

    mine = jnp.where((row64 >> 5) == ((lane64 >> 5) & 1), alpha_direct[:64], 0.0)
    part = alpha_energy - fold(mine[:32] + mine[32:], 32) * (1.0 / NK)
    a_out[...] = dot(gather8, jnp.where(lane_is_t, part, 0.0), precision=HIGH)
    send("col", X_ALPHA_COL, lambda peer: a_out, a_in)
    a_in[pl.ds(c, 1)] = a_out[...].reshape(1, 8, 128)

    arrived("col", X_DENS_COL, e_in)
    f_out[...] = jnp.sum(e_in[...], axis=0)
    send("row", X_DENS_OUT, lambda peer: f_out, f_in)
    f_in[pl.ds(r, 1)] = f_out[...].reshape(1, 8, 128)

    arrived("col", X_POT_COL, z_in)
    mixed = dot(perm_b[...], z_in[...].reshape(512, 128)).astype(BF16)
    y_out[...] = mixed.reshape(NR, NC, 128)
    send("row", X_POT_ROW, lambda peer: y_out.at[peer], y_in)
    y_in[pl.ds(r, 1)] = y_out[pl.ds(r, 1)]
    arrived("col", X_ALPHA_COL, a_in)
    b_out[...] = jnp.sum(a_in[...], axis=0)
    send("row", X_ALPHA_ROW, lambda peer: b_out, b_in)
    b_in[pl.ds(r, 1)] = b_out[...].reshape(1, 8, 128)

    arrived("row", X_DENS_OUT, f_in)
    density = f_in[...].reshape(256, 128)
    weighted = coulexp[...] * density
    w_hi, w_lo = split(weighted)
    quarters = pk[...]

    def total_of(v):
        v = jnp.where(own128, v, 0.0)
        return fold(v[0:32] + v[32:64] + v[64:96] + v[96:128], 64, 32)

    exchange = total_of(dot(quarters, w_hi) + dot(quarters, w_lo))
    alpha_exchange = total_of(dot(density, weighted, 0, 0, precision=HIGH))

    arrived("row", X_ALPHA_ROW, b_in)
    shares = dot(spread, jnp.sum(b_in[...], axis=0), precision=HIGH)
    shares = fold(jnp.where(lane_is_t, shares, 0.0), 64, 32)
    alpha = (shares + (2.0 / NT) * alpha_exchange) * (1.0 / NT)
    alpha_ref[...] = alpha[:, :32]
    base = ex128 + (2.0 / NT) * exchange - dot(x128[:, :32], alpha, precision=HIGH)

    arrived("row", X_POT_ROW, y_in)
    direct = jnp.where(own64, dot(lk[...], y_in[...].reshape(512, 128)), 0.0)
    residual = base - fold(direct[:32] + direct[32:], 64, 32) * (1.0 / NK)
    rows = dot(gather8, jnp.where(lane_is_t, residual, 0.0), precision=HIGH)
    for i in range(8):
        out_ref[i // 4 : i // 4 + 1, (i % 4) * 128 : (i % 4 + 1) * 128] = rows[i : i + 1, :]

    for axis, which, target in (
        ("row", X_COORD_ROW, k_in),
        ("row", X_PROJ_ROW, p_in),
        ("row", X_DENS_ROW, d_in),
        ("col", X_COORD_COL, h_in),
        ("col", X_PROJ_COL, q_in),
        ("col", X_DENS_COL, e_in),
        ("row", X_DENS_OUT, f_in),
        ("col", X_POT_COL, z_in),
        ("row", X_POT_ROW, y_in),
        ("col", X_ALPHA_COL, a_in),
        ("row", X_ALPHA_ROW, b_in),
    ):
        wait_all(axis, send_sems, which, target)


def on_device(pair_exchange, conduction, valence, coulomb, screening, energies, vectors, k_coords):
    q2, m_hi, m_lo = tables()
    vmem = pl.BlockSpec(memory_space=pltpu.VMEM)
    smem = pl.BlockSpec(memory_space=pltpu.SMEM)
    anywhere = pl.BlockSpec(memory_space=pl.ANY)
    return pl.pallas_call(
        kernel,
        out_shape=(
            jax.ShapeDtypeStruct((2, 512), F32),
            jax.ShapeDtypeStruct((32, 32), F32),
        ),
        in_specs=[vmem] * 6 + [smem, vmem] + [anywhere] * 3,
        out_specs=(vmem, vmem),
        scratch_shapes=[
            pltpu.VMEM((8, 128), F32),
            pltpu.VMEM((32, 1024), F32),
            pltpu.VMEM((64, 512), BF16),
            pltpu.VMEM((128, 256), BF16),
            pltpu.VMEM((256, 128), F32),
            pltpu.VMEM((8, 256), F32),
            pltpu.VMEM((NR, NC, 128), BF16),
            pltpu.VMEM((NR, NC, 128), BF16),
            pltpu.VMEM((NC, NR, 128), BF16),
            pltpu.VMEM((NC, NR, 128), BF16),
            pltpu.VMEM((NR, 8, 128), F32),
            pltpu.VMEM((NR, 8, 128), F32),
            pltpu.VMEM((8, 128), F32),
            pltpu.VMEM((NC, 8, 128), F32),
            pltpu.VMEM((8, 128), F32),
            pltpu.VMEM((NR, 8, 128), F32),
            pltpu.VMEM((1, 128), F32),
            pltpu.VMEM((NR, 1, 128), F32),
            pltpu.VMEM((1, 128), F32),
            pltpu.VMEM((NC, 1, 128), F32),
            pltpu.VMEM((16, 128), F32),
            pltpu.VMEM((NC, NR, 128), BF16),
            pltpu.VMEM((NC, NR, 128), BF16),
            pltpu.VMEM((NR, NC, 128), BF16),
            pltpu.VMEM((NR, NC, 128), BF16),
            pltpu.VMEM((8, 128), F32),
            pltpu.VMEM((NC, 8, 128), F32),
            pltpu.VMEM((8, 128), F32),
            pltpu.VMEM((NR, 8, 128), F32),
            pltpu.VMEM((2, 32, 512), F32),
            pltpu.VMEM((2, 32, 512), F32),
            pltpu.VMEM((2, NK, 512), BF16),
            pltpu.VMEM((2, NK, 512), BF16),
            pltpu.VMEM((NK, 128), F32),
            pltpu.VMEM((128, NK), BF16),
            pltpu.VMEM((512, 512), BF16),
            pltpu.VMEM((512, 512), BF16),
            pltpu.VMEM((2, QPAD, 128), F32),
            pltpu.VMEM((NK, QPAD), BF16),
            pltpu.VMEM((NK, QPAD), BF16),
            pltpu.SemaphoreType.DMA((11,)),
            pltpu.SemaphoreType.DMA((11,)),
            pltpu.SemaphoreType.DMA((4,)),
        ],
        compiler_params=pltpu.CompilerParams(
            collective_id=0, has_side_effects=True, vmem_limit_bytes=56 * 1024 * 1024
        ),
    )(
        pair_exchange,
        conduction,
        valence,
        coulomb.reshape(1, -1),
        energies,
        vectors,
        k_coords,
        jnp.asarray(q2),
        screening,
        jnp.asarray(m_hi),
        jnp.asarray(m_lo),
    )


def solution(mesh):
    split_k = ("row", "col")
    return jax.shard_map(
        on_device,
        mesh=mesh,
        in_specs=(
            P(split_k, None, None),
            P(split_k, None, None),
            P(split_k, None, None),
            P(),
            P(),
            P(split_k, None),
            P(split_k, None),
            P(split_k, None),
        ),
        out_specs=(P(split_k, None), P()),
        check_vma=False,
    )
```

time: 630 us -> 58.3 us (0.09); the launches traced: 623 us -> 58 us
  blocking collectives: 337 us -> 0 us
  local copies, waits for them, and re-layouts: 115 us -> 2.59 us
  waiting for transfers between devices: 79.3 us -> 0 us
  matrix products: 70.7 us -> 0 us
  Pallas kernels: 0 us -> 54.8 us
  between operations: 15.6 us -> 0.64 us
    all_gather x7 -> x0, blocking collectives: 267 us -> none  [the longest x1 42.1 us: on_device(): lax.all_gather(k_coords, ROW, axis=0, tiled=True)]
    reduce_scatter x1 -> x0, waiting for transfers between devices: 79.3 us -> none  [on_device(): lax.psum_scatter(forward.reshape(col_count, local_count, band_count, vect...]
    psum x5 -> x0, blocking collectives: 70.7 us -> none  [over_axes(): return functools.reduce(lax.psum, axes, x)]
    dot_general x28 -> x0, matrix products: 70.7 us -> none  [the longest x8 45.6 us: square_sweep(): jnp.einsum('ijg,jng->ing', coupling, col_proj, precision=highest)]
    gather x16 -> x0, local copies, waits for them, and re-layouts: 66.3 us -> none  [square_sweep(): jnp.take(lax.dynamic_slice_in_dim(screening, anchor, block_size, 1), indi...]
    pallas_call x0 -> x1, Pallas kernels: none -> 54.8 us  [on_device(): pl.pallas_call(kernel, out_shape=(jax.ShapeDtypeStruct((2, 512), F32), ja...]
    dot_general x8 -> x0, local copies, waits for them, and re-layouts: 23.2 us -> none  [square_sweep(): jnp.einsum('ktg,ktn->kng', col_block, col_moving, preferred_element_type=...]
    transpose x8 -> x0, local copies, waits for them, and re-layouts: 11.3 us -> none  [square_sweep(): jnp.einsum('ijg,jng->ing', coupling, col_proj, precision=highest)]
  transfers between devices with their start and end apart: 2 -> 0, of which waited for: 1 -> 0; matrix products, arithmetic and copies ran while one was open for 30% -> 0% of each run, Pallas kernels for 0% -> 0%
where the time goes in v1:
time: 58.3 us; the launch traced here: 58 us
  Pallas kernels  54.8 us (94%)
  local copies, waits for them, and re-layouts  2.59 us (4%)
  between operations  0.64 us (1%)
    pallas_call x1, Pallas kernels, on_device(): pl.pallas_call(kernel, out_shape=(jax.ShapeDtypeStruct((2, 512), F32), ja...  54.8 us
    unnamed x2, local copies, waits for them, and re-layouts  2.59 us

profile of v1, /device:TPU:1, one launch (start us, length us, event | category | flops | bytes accessed | tf_op | source)
XLA Modules:
  0.0 58.0 jit_solution(5783556098335171773)
XLA Ops:
  0.6 54.8 %shard_map.122 = (f32[2,512]{1,0:T(2,128)}, f32[32,32]{1,0:T(8,128)}) custom-call(bf16[2,16,1024]{2,1,0:T(8,128)(2,1)} %pe_ref.1, bf16[2,4,1024]{2,1,0:T(4,128)(2,1)} %cond_ref.1, bf16[2,4,1024]{2,1,0:T(4,128)(2,1)} %val_ref.1, f32[1,1024]{1,0:T(1,128)} %bitcast.1, f32[2,16]{1,0:T(2,128)} %en_ref.1, bf16[2,512]{1,0:T(2,128)(2,1)} %vec_ref.1, s32[2,2]{1,0:T(2,128)} %kc_ref.1, ...), custom_call_target="tpu_custom_call" | custom-call | tf_op jit(solution)/shard_map/pallas_call | solution.py:364
  55.4 1.3 %copy.15 = f32[2,512]{1,0:T(2,128)} copy(f32[2,512]{1,0:T(2,128)} %get-tuple-element.4) | data formatting | bytes 8192
  56.7 1.3 %copy.16 = f32[32,32]{1,0:T(8,128)} copy(f32[32,32]{1,0:T(8,128)} %get-tuple-element.5) | data formatting | bytes 8192

commit v2 on v1

--- a/solution.py
+++ b/solution.py
@@ -16,7 +16,7 @@
 NQ = 289
 QPAD = 384
 X_COORD_ROW, X_COORD_COL, X_PROJ_ROW, X_PROJ_COL, X_DENS_ROW, X_DENS_COL, X_DENS_OUT = range(7)
-X_POT_COL, X_POT_ROW, X_ALPHA_COL, X_ALPHA_ROW = range(7, 11)
+X_POT_COL, X_POT_ROW, X_ALPHA_ROW, X_ALPHA_COL = range(7, 11)
 
 
 def real_basis():
@@ -70,8 +70,9 @@
 
 
 def kernel(
-    pe_ref, cond_ref, val_ref, coul_ref, en_ref, vec_ref, kc_ref, q2_ref, scr_hbm, mhi_hbm, mlo_hbm,
+    pe_hbm, cond_hbm, val_hbm, coul_hbm, en_hbm, vec_hbm, kc_hbm, q2_hbm, scr_hbm, mhi_hbm, mlo_hbm,
     out_ref, alpha_ref,
+    pe_ref, cond_ref, val_ref, coul_ref, en_ref, vec_ref, kc_ref, q2_ref,
     v8, pairs, lk, pk, coulexp, c8,
     p_out, p_in, q_out, q_in, d_out, d_in, e_out, e_in, f_out, f_in,
     k_out, k_in, h_out, h_in, c16,
@@ -126,23 +127,28 @@
     near = pl.multiple_of((r // 8) * 128, 128)
     far = pl.multiple_of((r // 8) * 128 + 512, 128)
     fetches = [
-        pltpu.make_async_copy(
-            scr_hbm.at[:, pl.ds(near, 128)], scr.at[0, pl.ds(0, NQ), :], local_sems.at[0]
-        ),
-        pltpu.make_async_copy(
-            scr_hbm.at[:, pl.ds(far, 128)], scr.at[1, pl.ds(0, NQ), :], local_sems.at[1]
-        ),
-        pltpu.make_async_copy(mhi_hbm, m_hi, local_sems.at[2]),
-        pltpu.make_async_copy(mlo_hbm, m_lo, local_sems.at[3]),
+        pltpu.make_async_copy(source, target, local_sems.at[i])
+        for i, (source, target) in enumerate(
+            (
+                (vec_hbm, vec_ref),
+                (cond_hbm, cond_ref),
+                (val_hbm, val_ref),
+                (kc_hbm, kc_ref),
+                (pe_hbm, pe_ref),
+                (coul_hbm, coul_ref),
+                (en_hbm, en_ref),
+                (q2_hbm, q2_ref),
+                (scr_hbm.at[:, pl.ds(near, 128)], scr.at[0, pl.ds(0, NQ), :]),
+                (scr_hbm.at[:, pl.ds(far, 128)], scr.at[1, pl.ds(0, NQ), :]),
+                (mhi_hbm, m_hi),
+                (mlo_hbm, m_lo),
+            )
+        )
     ]
     for fetch in fetches:
         fetch.start()
-
-    place = iota((1, 128), 1) - 4 * r
-    k_row = jnp.zeros((1, 128), jnp.int32)
-    for q in range(4):
-        k_row = jnp.where(place == q, kc_ref[q // 2, q % 2], k_row)
-    k_out[...] = k_row.astype(F32)
+    for fetch in fetches[:3]:
+        fetch.wait()
 
     vec = vec_ref[...].astype(F32)
     for i in range(8):
@@ -168,6 +174,21 @@
     x_block = jnp.where(own64, jnp.concatenate([x128, x128], axis=0), 0.0).astype(BF16)
     p_out[...] = dot(lk[...], x_block, 0, 0).astype(BF16).reshape(NR, NC, 128)
 
+    pl.semaphore_wait(barrier, NR + NC - 2)
+    send("row", X_PROJ_ROW, lambda peer: p_out.at[peer], p_in)
+    p_in[pl.ds(r, 1)] = p_out[pl.ds(r, 1)]
+
+    for fetch in fetches[3:]:
+        fetch.wait()
+    place = iota((1, 128), 1) - 4 * r
+    k_row = jnp.zeros((1, 128), jnp.int32)
+    for q in range(4):
+        k_row = jnp.where(place == q, kc_ref[q // 2, q % 2], k_row)
+    k_out[...] = k_row.astype(F32)
+
+    send("row", X_COORD_ROW, lambda peer: k_out, k_in)
+    k_in[pl.ds(r, 1)] = k_out[...].reshape(1, 1, 128)
+
     for k in range(2):
         for j in range(4):
             at = 32 * j + 16 * k
@@ -176,12 +197,7 @@
     x_quarter = jnp.where(own128, jnp.concatenate([x128] * 4, axis=0), 0.0).astype(BF16)
     d_out[...] = dot(pk[...], x_quarter, 0, 0).reshape(NR, 8, 128)
 
-    pl.semaphore_wait(barrier, NR + NC - 2)
-    send("row", X_COORD_ROW, lambda peer: k_out, k_in)
-    send("row", X_PROJ_ROW, lambda peer: p_out.at[peer], p_in)
     send("row", X_DENS_ROW, lambda peer: d_out.at[peer], d_in)
-    k_in[pl.ds(r, 1)] = k_out[...].reshape(1, 1, 128)
-    p_in[pl.ds(r, 1)] = p_out[pl.ds(r, 1)]
     d_in[pl.ds(r, 1)] = d_out[pl.ds(r, 1)]
 
     def build_perm(i, carry):
@@ -211,8 +227,6 @@
     send("col", X_COORD_COL, lambda peer: h_out, h_in)
     h_in[pl.ds(c, 1)] = h_out[...].reshape(1, 1, 128)
 
-    for fetch in fetches:
-        fetch.wait()
     chosen = (r % 8) * 16 + c
     seen = (iota((QPAD, 128), 0) < NQ) & (iota((QPAD, 128), 1) == chosen)
     columns = [jnp.sum(jnp.where(seen, scr[h], 0.0), axis=1, keepdims=True) for h in range(2)]
@@ -285,9 +299,7 @@
     for k in range(2):
         both = dot(wt[...], tt_hi[k])
         back = both[:64] + both[64:] + dot(wt[0:64, :], tt_lo[k])
-        coords_free = jnp.transpose(back)
-        brow_at = 64 * k
-        lam[0:512, brow_at : brow_at + 64] = coords_free
+        lam[0:512, 64 * k : 64 * k + 64] = jnp.transpose(back)
     z_out[...] = lam[0:512, :].astype(BF16).reshape(NC, NR, 128)
     send("col", X_POT_COL, lambda peer: z_out.at[peer], z_in)
     z_in[pl.ds(c, 1)] = z_out[pl.ds(c, 1)]
@@ -295,8 +307,8 @@
     mine = jnp.where((row64 >> 5) == ((lane64 >> 5) & 1), alpha_direct[:64], 0.0)
     part = alpha_energy - fold(mine[:32] + mine[32:], 32) * (1.0 / NK)
     a_out[...] = dot(gather8, jnp.where(lane_is_t, part, 0.0), precision=HIGH)
-    send("col", X_ALPHA_COL, lambda peer: a_out, a_in)
-    a_in[pl.ds(c, 1)] = a_out[...].reshape(1, 8, 128)
+    send("row", X_ALPHA_ROW, lambda peer: a_out, a_in)
+    a_in[pl.ds(r, 1)] = a_out[...].reshape(1, 8, 128)
 
     arrived("col", X_DENS_COL, e_in)
     f_out[...] = jnp.sum(e_in[...], axis=0)
@@ -308,10 +320,10 @@
     y_out[...] = mixed.reshape(NR, NC, 128)
     send("row", X_POT_ROW, lambda peer: y_out.at[peer], y_in)
     y_in[pl.ds(r, 1)] = y_out[pl.ds(r, 1)]
-    arrived("col", X_ALPHA_COL, a_in)
+    arrived("row", X_ALPHA_ROW, a_in)
     b_out[...] = jnp.sum(a_in[...], axis=0)
-    send("row", X_ALPHA_ROW, lambda peer: b_out, b_in)
-    b_in[pl.ds(r, 1)] = b_out[...].reshape(1, 8, 128)
+    send("col", X_ALPHA_COL, lambda peer: b_out, b_in)
+    b_in[pl.ds(c, 1)] = b_out[...].reshape(1, 8, 128)
 
     arrived("row", X_DENS_OUT, f_in)
     density = f_in[...].reshape(256, 128)
@@ -326,7 +338,7 @@
     exchange = total_of(dot(quarters, w_hi) + dot(quarters, w_lo))
     alpha_exchange = total_of(dot(density, weighted, 0, 0, precision=HIGH))
 
-    arrived("row", X_ALPHA_ROW, b_in)
+    arrived("col", X_ALPHA_COL, b_in)
     shares = dot(spread, jnp.sum(b_in[...], axis=0), precision=HIGH)
     shares = fold(jnp.where(lane_is_t, shares, 0.0), 64, 32)
     alpha = (shares + (2.0 / NT) * alpha_exchange) * (1.0 / NT)
@@ -350,26 +362,36 @@
         ("row", X_DENS_OUT, f_in),
         ("col", X_POT_COL, z_in),
         ("row", X_POT_ROW, y_in),
-        ("col", X_ALPHA_COL, a_in),
-        ("row", X_ALPHA_ROW, b_in),
+        ("row", X_ALPHA_ROW, a_in),
+        ("col", X_ALPHA_COL, b_in),
     ):
         wait_all(axis, send_sems, which, target)
 
 
 def on_device(pair_exchange, conduction, valence, coulomb, screening, energies, vectors, k_coords):
-    q2, m_hi, m_lo = tables()
+    q2, m_hi, m_lo = (jnp.asarray(table) for table in tables())
+    operands = (
+        *(pair_exchange, conduction, valence, coulomb.reshape(1, -1), energies, vectors, k_coords),
+        *(q2, screening, m_hi, m_lo),
+    )
     vmem = pl.BlockSpec(memory_space=pltpu.VMEM)
-    smem = pl.BlockSpec(memory_space=pltpu.SMEM)
-    anywhere = pl.BlockSpec(memory_space=pl.ANY)
     return pl.pallas_call(
         kernel,
         out_shape=(
             jax.ShapeDtypeStruct((2, 512), F32),
             jax.ShapeDtypeStruct((32, 32), F32),
         ),
-        in_specs=[vmem] * 6 + [smem, vmem] + [anywhere] * 3,
+        in_specs=[pl.BlockSpec(memory_space=pltpu.HBM)] * 11,
         out_specs=(vmem, vmem),
         scratch_shapes=[
+            pltpu.VMEM((2, 16, 1024), BF16),
+            pltpu.VMEM((2, 4, 1024), BF16),
+            pltpu.VMEM((2, 4, 1024), BF16),
+            pltpu.VMEM((1, 1024), F32),
+            pltpu.VMEM((2, 16), F32),
+            pltpu.VMEM((2, 512), BF16),
+            pltpu.SMEM((2, 2), jnp.int32),
+            pltpu.VMEM((32, 64), BF16),
             pltpu.VMEM((8, 128), F32),
             pltpu.VMEM((32, 1024), F32),
             pltpu.VMEM((64, 512), BF16),
@@ -396,9 +418,9 @@
             pltpu.VMEM((NR, NC, 128), BF16),
             pltpu.VMEM((NR, NC, 128), BF16),
             pltpu.VMEM((8, 128), F32),
+            pltpu.VMEM((NR, 8, 128), F32),
+            pltpu.VMEM((8, 128), F32),
             pltpu.VMEM((NC, 8, 128), F32),
-            pltpu.VMEM((8, 128), F32),
-            pltpu.VMEM((NR, 8, 128), F32),
             pltpu.VMEM((2, 32, 512), F32),
             pltpu.VMEM((2, 32, 512), F32),
             pltpu.VMEM((2, NK, 512), BF16),
@@ -412,24 +434,12 @@
             pltpu.VMEM((NK, QPAD), BF16),
             pltpu.SemaphoreType.DMA((11,)),
             pltpu.SemaphoreType.DMA((11,)),
-            pltpu.SemaphoreType.DMA((4,)),
+            pltpu.SemaphoreType.DMA((12,)),
         ],
         compiler_params=pltpu.CompilerParams(
-            collective_id=0, has_side_effects=True, vmem_limit_bytes=56 * 1024 * 1024
+            collective_id=0, has_side_effects=True, vmem_limit_bytes=24 * 1024 * 1024
         ),
-    )(
-        pair_exchange,
-        conduction,
-        valence,
-        coulomb.reshape(1, -1),
-        energies,
-        vectors,
-        k_coords,
-        jnp.asarray(q2),
-        screening,
-        jnp.asarray(m_hi),
-        jnp.asarray(m_lo),
-    )
+    )(*(pltpu.with_memory_space_constraint(v, pltpu.HBM) for v in operands))
 
 
 def solution(mesh):

time: 58.3 us -> 54.4 us (0.933)
  Pallas kernels: 54.8 us -> 52.1 us
  local copies, waits for them, and re-layouts: 2.59 us -> 1.2 us
    pallas_call x1, Pallas kernels: 54.8 us -> 52.1 us  [on_device(): pl.pallas_call(kernel, out_shape=(jax.ShapeDtypeStruct((2, 512), F32), ja...]
    unnamed x2, local copies, waits for them, and re-layouts: 2.59 us -> 1.2 us
where the time goes in v2:
time: 54.4 us; the launch traced here: 54 us
  Pallas kernels  52.1 us (96%)
  local copies, waits for them, and re-layouts  1.2 us (2%)
  between operations  0.64 us (1%)
    pallas_call x1, Pallas kernels, on_device(): pl.pallas_call(kernel, out_shape=(jax.ShapeDtypeStruct((2, 512), F32), ja...  52.1 us
    unnamed x2, local copies, waits for them, and re-layouts  1.2 us

profile of v2, /device:TPU:1, one launch (start us, length us, event | category | flops | bytes accessed | tf_op | source)
XLA Modules:
  0.0 54.0 jit_solution(8847640238486847342)
XLA Ops:
  0.6 52.1 %shard_map.122 = (f32[2,512]{1,0:T(2,128)S(1)}, f32[32,32]{1,0:T(8,128)S(1)}) custom-call(bf16[2,16,1024]{2,1,0:T(8,128)(2,1)} %pe_hbm.1, bf16[2,4,1024]{2,1,0:T(4,128)(2,1)} %cond_hbm.1, bf16[2,4,1024]{2,1,0:T(4,128)(2,1)} %val_hbm.1, f32[1,1024]{1,0:T(1,128)} %bitcast.1, f32[2,16]{1,0:T(2,128)} %en_hbm.1, bf16[2,512]{1,0:T(2,128)(2,1)} %vec_hbm.1, ...), custom_call_target="tpu_custom_call" | custom-call | tf_op jit(solution)/shard_map/pallas_call | solution.py:378
  52.8 0.6 %copy.15 = f32[2,512]{1,0:T(2,128)} copy(f32[2,512]{1,0:T(2,128)S(1)} %get-tuple-element.4) | data formatting | bytes 8192
  53.4 0.6 %copy.16 = f32[32,32]{1,0:T(8,128)} copy(f32[32,32]{1,0:T(8,128)S(1)} %get-tuple-element.5) | data formatting | bytes 8192

commit v3 on v2

v3 whole, which is shorter than its diff:
```python
import jax
import jax.numpy as jnp
import numpy as np
from jax import lax
from jax.experimental import pallas as pl
from jax.experimental.pallas import tpu as pltpu
from jax.sharding import PartitionSpec as P

MESH = pl.DeviceIdType.MESH
HIGH = lax.Precision.HIGHEST
F32 = jnp.float32
BF16 = jnp.bfloat16

NR, NC, NU = 32, 16, 16
NK, NT = 1024, 16384
NQ = 289
QPAD = 384
COORD_ROW, COORD_COL, PROJ_ROW, PROJ_COL, POT_COL, POT_ROW = range(6)
DENS_PAIR, DENS_ROW, DENS_COL, DENS_OUT, DENS_SWAP = range(6, 11)
ALPHA_PAIR, ALPHA_ROW, ALPHA_COL, ALPHA_SWAP = range(11, 15)


def real_basis():
    points = np.arange(32)[None, :]
    order = np.arange(32)[:, None]
    freq = np.where(order <= 16, order, order - 16)
    angle = 2 * np.pi * freq * points / 32
    basis = np.where(order <= 16, np.cos(angle), np.sin(angle)) * np.sqrt(2 / 32)
    basis[[0, 16]] *= np.sqrt(0.5)
    return basis, freq[:, 0]


def two_parts(table):
    high = table.astype(BF16)
    return high, (table - high.astype(np.float64)).astype(BF16)


def tables():
    basis, freq = real_basis()
    fold = np.arange(17)
    weight = np.where((fold == 0) | (fold == 16), 1.0, 2.0)
    cosine = weight[None, :] * np.cos(2 * np.pi * freq[:, None] * fold[None, :] / 32)
    modes = np.zeros((QPAD, NK))
    modes[:NQ] = np.kron(cosine, cosine).T
    narrow = np.concatenate(two_parts(basis), axis=1)
    outer = np.concatenate(two_parts(np.repeat(basis.T, 32, axis=1)), axis=0)
    inner = np.concatenate(two_parts(np.tile(basis.T, (1, 32))), axis=0)
    return narrow, outer, inner, *two_parts(modes)


def iota(shape, dim):
    return lax.broadcasted_iota(jnp.int32, shape, dim)


def one_hot(mask):
    return jnp.where(mask, 1.0, 0.0).astype(F32)


def dot(a, b, ca=1, cb=0, precision=None):
    return lax.dot_general(
        a, b, (((ca,), (cb,)), ((), ())), precision=precision, preferred_element_type=F32
    )


def split(v):
    high = v.astype(BF16)
    return high, (v - high.astype(F32)).astype(BF16)


def fold(v, *shifts):
    for shift in shifts:
        v = v + pltpu.roll(v, shift, 1)
    return v


def kernel(
    pe_hbm, cond_hbm, val_hbm, coul_hbm, en_hbm, vec_hbm, kc_hbm, q2_hbm, qa_hbm, qb_hbm, scr_hbm,
    mhi_hbm, mlo_hbm,
    out_ref, alpha_ref,
    pe_ref, cond_ref, val_ref, coul_ref, en_ref, vec_ref, kc_ref, q2_ref, qa_ref, qb_ref,
    v8, pairs, lk, pk, coulexp, c8,
    p_out, p_in, q_out, q_in, z_out, z_in, y_out, y_in,
    k_out, k_in, h_out, h_in, c16,
    d_out, d_pair, d_sum, d_in, e_out, e_in, f_out, f_in,
    a_out, a_pair, b_out, b_in, g_out, g_in, a_full,
    arow, brow, t_all, tt_hi, tt_lo, lam, wt, z_wide, perm_f, perm_b, scr, m_hi, m_lo,
    send_sems, recv_sems, local_sems,
):
    r, c = lax.axis_index("row"), lax.axis_index("col")
    core, chip = lax.rem(r, 2), r // 2
    groups = {"row": (NR, r), "col": (NC, c), "chip": (NU, chip)}

    def device(group, peer):
        if group == "chip":
            return {"row": 2 * peer + core}
        return {group: peer}

    def peers(group, body):
        size, me = groups[group]
        half = size // 2

        def step(i, carry):
            ahead = jnp.where(i < half, half + i, i - half + 1)
            body(lax.rem(me + ahead, size))
            return carry

        lax.fori_loop(0, size - 1, step, 0)

    def copy_to(device_id, which, source, target):
        return pltpu.make_async_remote_copy(
            src_ref=source,
            dst_ref=target,
            send_sem=send_sems.at[which],
            recv_sem=recv_sems.at[which],
            device_id=device_id,
            device_id_type=MESH,
        )

    def send(group, which, source, target, base=0):
        slot = base + groups[group][1]
        peers(
            group,
            lambda peer: copy_to(
                device(group, peer), which, source(peer), target.at[slot]
            ).start(),
        )

    def wait_bytes(sem, many):
        pltpu.make_async_copy(many, many, sem).wait()

    waits = []

    def arrived(group, which, target):
        many = target.at[pl.ds(0, groups[group][0] - 1)]
        waits.append((which, many))
        wait_bytes(recv_sems.at[which], many)

    def arrived_pair(which, target):
        waits.append((which, target))
        wait_bytes(recv_sems.at[which], target)

    sibling = {"row": r + 1 - 2 * core}

    barrier = pltpu.get_barrier_semaphore()
    for axis in ("row", "col"):
        peers(
            axis,
            lambda peer, axis=axis: pl.semaphore_signal(
                barrier, inc=1, device_id={axis: peer}, device_id_type=MESH
            ),
        )
    near = pl.multiple_of((r // 8) * 128, 128)
    far = pl.multiple_of((r // 8) * 128 + 512, 128)
    fetches = [
        pltpu.make_async_copy(source, target, local_sems.at[i])
        for i, (source, target) in enumerate(
            (
                (vec_hbm, vec_ref),
                (cond_hbm, cond_ref),
                (val_hbm, val_ref),
                (kc_hbm, kc_ref),
                (pe_hbm, pe_ref),
                (coul_hbm, coul_ref),
                (en_hbm, en_ref),
                (q2_hbm, q2_ref),
                (scr_hbm.at[:, pl.ds(near, 128)], scr.at[0, pl.ds(0, NQ), :]),
                (scr_hbm.at[:, pl.ds(far, 128)], scr.at[1, pl.ds(0, NQ), :]),
                (mhi_hbm, m_hi),
                (mlo_hbm, m_lo),
                (qa_hbm, qa_ref),
                (qb_hbm, qb_ref),
            )
        )
    ]
    for fetch in fetches:
        fetch.start()
    for fetch in fetches[:3]:
        fetch.wait()

    vec = vec_ref[...].astype(F32)
    for i in range(8):
        v8[i : i + 1, :] = vec[i // 4 : i // 4 + 1, (i % 4) * 128 : (i % 4 + 1) * 128]
    row32, lane32 = iota((32, 128), 0), iota((32, 128), 1)
    lane_is_t = (row32 & 3) == (lane32 >> 5)
    spread = one_hot((iota((32, 8), 0) >> 2) == iota((32, 8), 1))
    gather8 = one_hot((iota((8, 32), 1) >> 2) == iota((8, 32), 0))
    wide = dot(spread.astype(BF16), v8[...].astype(BF16))
    x128 = fold(jnp.where(lane_is_t, wide, 0.0), 64, 32)

    for k in range(2):
        cond = cond_ref[k].astype(F32)
        val = val_ref[k].astype(F32)
        for v in range(4):
            at = 16 * k + 4 * v
            pairs[at : at + 4, :] = val[v : v + 1, :] * cond
    pair_rows = pairs[...].astype(BF16)
    lk[0:32, :] = pair_rows[:, :512]
    lk[32:64, :] = pair_rows[:, 512:]
    row64, lane64 = iota((64, 128), 0), iota((64, 128), 1)
    own64 = ((row64 >> 5) == ((lane64 >> 5) & 1)) & (((row64 >> 4) & 1) == (lane64 >> 6))
    x_block = jnp.where(own64, jnp.concatenate([x128, x128], axis=0), 0.0).astype(BF16)
    p_out[...] = dot(lk[...], x_block, 0, 0).astype(BF16).reshape(NR, NC, 128)

    for fetch in fetches[3:8]:
        fetch.wait()
    place = iota((1, 128), 1) - 4 * r
    k_row = jnp.zeros((1, 128), jnp.int32)
    for q in range(4):
        k_row = jnp.where(place == q, kc_ref[q // 2, q % 2], k_row)
    k_out[...] = k_row.astype(F32)

    pl.semaphore_wait(barrier, NR + NC - 2)
    send("row", COORD_ROW, lambda peer: k_out, k_in)
    send("row", PROJ_ROW, lambda peer: p_out.at[peer], p_in)
    k_in[pl.ds(r, 1)] = k_out[...].reshape(1, 1, 128)
    p_in[pl.ds(r, 1)] = p_out[pl.ds(r, 1)]

    for k in range(2):
        for j in range(4):
            at = 32 * j + 16 * k
            pk[at : at + 16, :] = pe_ref[k, :, j * 256 : (j + 1) * 256]
    own128 = (iota((128, 128), 0) >> 5) == (iota((128, 128), 1) >> 5)
    x_quarter = jnp.where(own128, jnp.concatenate([x128] * 4, axis=0), 0.0).astype(BF16)
    d_out[...] = dot(pk[...], x_quarter, 0, 0).reshape(NR, 8, 128)
    mine = pl.multiple_of(core * NU, NU)
    other = pl.multiple_of(NU - core * NU, NU)
    copy_to(sibling, DENS_PAIR, d_out.at[pl.ds(other, NU)], d_pair).start()

    def build_perm(i, carry):
        at = pl.multiple_of(i * 128, 128)
        row, col = iota((128, 512), 0) + i * 128, iota((128, 512), 1)
        perm_f[pl.ds(at, 128), :] = one_hot(col == ((row & 31) << 4) + (row >> 5)).astype(BF16)
        perm_b[pl.ds(at, 128), :] = one_hot(col == ((row & 15) << 5) + (row >> 4)).astype(BF16)
        return carry

    lax.fori_loop(0, 4, build_perm, 0)

    arrived_pair(DENS_PAIR, d_pair)
    d_sum[...] = d_out[pl.ds(mine, NU)] + d_pair[...]
    send("chip", DENS_ROW, lambda peer: d_sum.at[peer], d_in)
    d_in[pl.ds(chip, 1)] = d_sum[pl.ds(chip, 1)]

    for fetch in fetches[8:]:
        fetch.wait()
    chosen = lax.rem(r, 8) * 16 + c
    q_row, q_lane = iota((8, 128), 0), iota((8, 128), 1)
    known = iota((QPAD, 128), 0) < NQ
    values = sum(
        dot(
            one_hot((q_row == h) & (q_lane == chosen)),
            jnp.where(known, scr[h], 0.0),
            1,
            1,
            precision=HIGH,
        )
        for h in range(2)
    )
    s_hi, s_lo = split(values)
    lam[...] = dot(s_hi, m_hi[...]) + dot(s_lo, m_hi[...]) + dot(s_hi, m_lo[...])

    arrived("row", COORD_ROW, k_in)
    h_out[...] = jnp.sum(k_in[...], axis=0)
    send("col", COORD_COL, lambda peer: h_out, h_in)
    h_in[pl.ds(c, 1)] = h_out[...].reshape(1, 1, 128)

    arrived("row", PROJ_ROW, p_in)
    mixed = dot(perm_f[...], p_in[...].reshape(512, 128)).astype(BF16)
    q_out[...] = mixed.reshape(NC, NR, 128)
    send("col", PROJ_COL, lambda peer: q_out.at[peer], q_in)
    q_in[pl.ds(c, 1)] = q_out[pl.ds(c, 1)]
    arrived("chip", DENS_ROW, d_in)
    e_out[...] = jnp.sum(d_in[...], axis=0)
    send("col", DENS_COL, lambda peer: e_out, e_in)
    e_in[pl.ds(c, 1)] = e_out[...].reshape(1, 8, 128)

    arrived("col", COORD_COL, h_in)
    for i in range(NC):
        c16[i : i + 1, :] = h_in[i]
    repeat = one_hot(iota((16, 512), 0) == (iota((16, 512), 1) >> 5)).astype(BF16)
    spread_c = dot(c16[...].astype(BF16), repeat, 0, 0)
    row128, lane512 = iota((128, 512), 0), iota((128, 512), 1)
    kept = jnp.where((row128 >> 2) == (lane512 & 31), spread_c, 0.0).astype(BF16)
    pick = one_hot((iota((128, 128), 0) >> 5) == (iota((128, 128), 1) & 3)).astype(BF16)
    coords = dot(pick, kept)
    hot = one_hot(coords == (row128 & 31).astype(F32)).astype(BF16)
    q2 = q2_ref[...]
    for k in range(2):
        at = 64 * k
        first = jnp.concatenate([hot[at : at + 32]] * 2, axis=0)
        second = jnp.concatenate([hot[at + 32 : at + 64]] * 2, axis=0)
        arow[k] = dot(q2, first)
        brow[k] = dot(q2, second)
        for i in range(4):
            at = 128 * i
            outer = dot(first[:, at : at + 128], qa_ref[...], 0, 0)
            inner = dot(second[:, at : at + 128], qb_ref[...], 0, 0)
            high, low = split(outer * inner)
            t_all[512 * k + at : 512 * k + at + 128, :] = high
            t_all[1024 + 512 * k + at : 1024 + 512 * k + at + 128, :] = low

    def build_basis(j, carry):
        at = pl.multiple_of(j * 32, 32)
        for k in range(2):
            high, low = split(arow[k, pl.ds(j, 1), :] * brow[k])
            tt_hi[k, pl.ds(at, 32), :] = high
            tt_lo[k, pl.ds(at, 32), :] = low
        return carry

    lax.fori_loop(0, 32, build_basis, 0)

    arrived("col", PROJ_COL, q_in)
    turned = jnp.transpose(q_in[...].reshape(512, 128).astype(F32)).astype(BF16)
    mode = dot(jnp.concatenate([turned[:64], turned[64:]] * 2, axis=1), t_all[...])
    first_g = iota((64, NK), 0) < 32
    scaled = jnp.where(first_g, lam[0:1, :], lam[1:2, :]) * mode
    high, low = split(scaled)
    wt[0:64, :] = high
    wt[64:128, :] = low
    for k in range(2):
        both = dot(wt[...], tt_hi[k])
        back = both[:64] + both[64:] + dot(wt[0:64, :], tt_lo[k])
        z_wide[64 * k : 64 * k + 64, :] = back
    z_out[...] = jnp.transpose(z_wide[...]).astype(BF16).reshape(NC, NR, 128)
    send("col", POT_COL, lambda peer: z_out.at[peer], z_in)
    z_in[pl.ds(c, 1)] = z_out[pl.ds(c, 1)]

    energy = jnp.concatenate(
        [jnp.broadcast_to(en_ref[k : k + 1, :], (16, 16)) for k in range(2)], axis=0
    )
    same = (iota((32, 16), 0) & 15) == iota((32, 16), 1)
    e_col = jnp.sum(jnp.where(same, energy, 0.0), axis=1, keepdims=True)
    ex128 = e_col * x128
    alpha_energy = dot(x128, ex128, 0, 0, precision=HIGH)[:32]
    alpha_direct = dot(mode.astype(BF16), jnp.concatenate([high, high], axis=0), 1, 1)
    kept_g = jnp.where((row64 >> 5) == ((lane64 >> 5) & 1), alpha_direct, 0.0)
    part = alpha_energy - fold(kept_g[:32] + kept_g[32:], 32) * (1.0 / NK)
    packed = dot(gather8, jnp.where(lane_is_t, part, 0.0), precision=HIGH)
    a_out[0] = packed[0:4]
    a_out[1] = packed[4:8]
    copy_to(sibling, ALPHA_PAIR, a_out.at[1 - core], a_pair.at[0]).start()

    arrived("col", DENS_COL, e_in)
    f_out[...] = jnp.sum(e_in[...], axis=0)
    send("chip", DENS_OUT, lambda peer: f_out, f_in, base=mine)
    f_in[pl.ds(mine + chip, 1)] = f_out[...].reshape(1, 8, 128)

    arrived_pair(ALPHA_PAIR, a_pair)
    b_out[...] = a_out[pl.ds(core, 1)] + a_pair[...]
    send("chip", ALPHA_ROW, lambda peer: b_out.at[0], b_in)
    b_in[pl.ds(chip, 1)] = b_out[...]

    c8[...] = jnp.zeros((8, 256), F32)
    for j in range(4):
        c8[j : j + 1, :] = coul_ref[:, j * 256 : (j + 1) * 256]
    expand8 = one_hot(iota((8, 128), 0) == (iota((8, 128), 1) >> 5))
    coulexp[...] = dot(c8[...], expand8, 0, 0, precision=HIGH)

    arrived("col", POT_COL, z_in)
    mixed = dot(perm_b[...], z_in[...].reshape(512, 128)).astype(BF16)
    y_out[...] = mixed.reshape(NR, NC, 128)
    send("row", POT_ROW, lambda peer: y_out.at[peer], y_in)
    y_in[pl.ds(r, 1)] = y_out[pl.ds(r, 1)]

    arrived("chip", ALPHA_ROW, b_in)
    g_out[...] = jnp.sum(b_in[...], axis=0, keepdims=True)
    send("col", ALPHA_COL, lambda peer: g_out.at[0], g_in)
    g_in[pl.ds(c, 1)] = g_out[...]

    arrived("chip", DENS_OUT, f_in)
    half = f_in.at[pl.ds(mine, NU)]
    copy_to(sibling, DENS_SWAP, half, half).start()
    arrived_pair(DENS_SWAP, f_in.at[pl.ds(other, NU)])
    density = f_in[...].reshape(256, 128)
    weighted = coulexp[...] * density
    w_hi, w_lo = split(weighted)
    quarters = pk[...]

    def total_of(v):
        v = jnp.where(own128, v, 0.0)
        return fold(v[0:32] + v[32:64] + v[64:96] + v[96:128], 64, 32)

    exchange = total_of(dot(quarters, w_hi) + dot(quarters, w_lo))
    alpha_exchange = total_of(dot(density, weighted, 0, 0, precision=HIGH))

    arrived("col", ALPHA_COL, g_in)
    a_full[pl.ds(core, 1)] = jnp.sum(g_in[...], axis=0, keepdims=True)
    copy_to(sibling, ALPHA_SWAP, a_full.at[core], a_full.at[core]).start()
    arrived_pair(ALPHA_SWAP, a_full.at[1 - core])
    shares = dot(spread[:, 0:4], a_full[0], precision=HIGH)
    shares = shares + dot(spread[:, 4:8], a_full[1], precision=HIGH)
    shares = fold(jnp.where(lane_is_t, shares, 0.0), 64, 32)
    alpha = (shares + (2.0 / NT) * alpha_exchange) * (1.0 / NT)
    alpha_ref[...] = alpha[:, :32]
    base = ex128 + (2.0 / NT) * exchange - dot(x128[:, :32], alpha, precision=HIGH)

    arrived("row", POT_ROW, y_in)
    direct = jnp.where(own64, dot(lk[...], y_in[...].reshape(512, 128)), 0.0)
    residual = base - fold(direct[:32] + direct[32:], 64, 32) * (1.0 / NK)
    rows = dot(gather8, jnp.where(lane_is_t, residual, 0.0), precision=HIGH)
    for i in range(8):
        out_ref[i // 4 : i // 4 + 1, (i % 4) * 128 : (i % 4 + 1) * 128] = rows[i : i + 1, :]

    for which, many in waits:
        wait_bytes(send_sems.at[which], many)


def on_device(pair_exchange, conduction, valence, coulomb, screening, energies, vectors, k_coords):
    q2, qa, qb, m_hi, m_lo = (jnp.asarray(table) for table in tables())
    operands = (
        *(pair_exchange, conduction, valence, coulomb.reshape(1, -1), energies, vectors, k_coords),
        *(q2, qa, qb, screening, m_hi, m_lo),
    )
    vmem = pl.BlockSpec(memory_space=pltpu.VMEM)
    return pl.pallas_call(
        kernel,
        out_shape=(
            jax.ShapeDtypeStruct((2, 512), F32),
            jax.ShapeDtypeStruct((32, 32), F32),
        ),
        in_specs=[pl.BlockSpec(memory_space=pltpu.HBM)] * len(operands),
        out_specs=(vmem, vmem),
        scratch_shapes=[
            pltpu.VMEM((2, 16, 1024), BF16),
            pltpu.VMEM((2, 4, 1024), BF16),
            pltpu.VMEM((2, 4, 1024), BF16),
            pltpu.VMEM((1, 1024), F32),
            pltpu.VMEM((2, 16), F32),
            pltpu.VMEM((2, 512), BF16),
            pltpu.SMEM((2, 2), jnp.int32),
            pltpu.VMEM((32, 64), BF16),
            pltpu.VMEM((64, NK), BF16),
            pltpu.VMEM((64, NK), BF16),
            pltpu.VMEM((8, 128), F32),
            pltpu.VMEM((32, 1024), F32),
            pltpu.VMEM((64, 512), BF16),
            pltpu.VMEM((128, 256), BF16),
            pltpu.VMEM((256, 128), F32),
            pltpu.VMEM((8, 256), F32),
            pltpu.VMEM((NR, NC, 128), BF16),
            pltpu.VMEM((NR, NC, 128), BF16),
            pltpu.VMEM((NC, NR, 128), BF16),
            pltpu.VMEM((NC, NR, 128), BF16),
            pltpu.VMEM((NC, NR, 128), BF16),
            pltpu.VMEM((NC, NR, 128), BF16),
            pltpu.VMEM((NR, NC, 128), BF16),
            pltpu.VMEM((NR, NC, 128), BF16),
            pltpu.VMEM((1, 128), F32),
            pltpu.VMEM((NR, 1, 128), F32),
            pltpu.VMEM((1, 128), F32),
            pltpu.VMEM((NC, 1, 128), F32),
            pltpu.VMEM((16, 128), F32),
            pltpu.VMEM((NR, 8, 128), F32),
            pltpu.VMEM((NU, 8, 128), F32),
            pltpu.VMEM((NU, 8, 128), F32),
            pltpu.VMEM((NU, 8, 128), F32),
            pltpu.VMEM((8, 128), F32),
            pltpu.VMEM((NC, 8, 128), F32),
            pltpu.VMEM((8, 128), F32),
            pltpu.VMEM((NR, 8, 128), F32),
            pltpu.VMEM((2, 4, 128), F32),
            pltpu.VMEM((1, 4, 128), F32),
            pltpu.VMEM((1, 4, 128), F32),
            pltpu.VMEM((NU, 4, 128), F32),
            pltpu.VMEM((1, 4, 128), F32),
            pltpu.VMEM((NC, 4, 128), F32),
            pltpu.VMEM((2, 4, 128), F32),
            pltpu.VMEM((2, 32, 512), F32),
            pltpu.VMEM((2, 32, 512), F32),
            pltpu.VMEM((2048, NK), BF16),
            pltpu.VMEM((2, NK, 512), BF16),
            pltpu.VMEM((2, NK, 512), BF16),
            pltpu.VMEM((8, NK), F32),
            pltpu.VMEM((128, NK), BF16),
            pltpu.VMEM((128, 512), F32),
            pltpu.VMEM((512, 512), BF16),
            pltpu.VMEM((512, 512), BF16),
            pltpu.VMEM((2, QPAD, 128), F32),
            pltpu.VMEM((QPAD, NK), BF16),
            pltpu.VMEM((QPAD, NK), BF16),
            pltpu.SemaphoreType.DMA((15,)),
            pltpu.SemaphoreType.DMA((15,)),
            pltpu.SemaphoreType.DMA((14,)),
        ],
        compiler_params=pltpu.CompilerParams(
            collective_id=0, has_side_effects=True, vmem_limit_bytes=32 * 1024 * 1024
        ),
    )(*(pltpu.with_memory_space_constraint(v, pltpu.HBM) for v in operands))


def solution(mesh):
    split_k = ("row", "col")
    return jax.shard_map(
        on_device,
        mesh=mesh,
        in_specs=(
            P(split_k, None, None),
            P(split_k, None, None),
            P(split_k, None, None),
            P(),
            P(),
            P(split_k, None),
            P(split_k, None),
            P(split_k, None),
        ),
        out_specs=(P(split_k, None), P()),
        check_vma=False,
    )
```

time: 54.4 us -> 52.1 us (0.958)
  Pallas kernels: 52.1 us -> 50.1 us
    pallas_call x1, Pallas kernels: 52.1 us -> 50.1 us  [on_device(): pl.pallas_call(kernel, out_shape=(jax.ShapeDtypeStruct((2, 512), F32), ja...]
where the time goes in v3:
time: 52.1 us; the launch traced here: 52 us
  Pallas kernels  50.1 us (96%)
  local copies, waits for them, and re-layouts  1.2 us (2%)
  between operations  0.64 us (1%)
    pallas_call x1, Pallas kernels, on_device(): pl.pallas_call(kernel, out_shape=(jax.ShapeDtypeStruct((2, 512), F32), ja...  50.1 us
    unnamed x2, local copies, waits for them, and re-layouts  1.2 us

profile of v3, /device:TPU:1, one launch (start us, length us, event | category | flops | bytes accessed | tf_op | source)
XLA Modules:
  0.0 52.0 jit_solution(1531426060580421695)
XLA Ops:
  0.6 50.1 %shard_map.140 = (f32[2,512]{1,0:T(2,128)S(1)}, f32[32,32]{1,0:T(8,128)S(1)}) custom-call(bf16[2,16,1024]{2,1,0:T(8,128)(2,1)} %pe_hbm.1, bf16[2,4,1024]{2,1,0:T(4,128)(2,1)} %cond_hbm.1, bf16[2,4,1024]{2,1,0:T(4,128)(2,1)} %val_hbm.1, f32[1,1024]{1,0:T(1,128)} %bitcast.1, f32[2,16]{1,0:T(2,128)} %en_hbm.1, bf16[2,512]{1,0:T(2,128)(2,1)} %vec_hbm.1, ...), custom_call_target="tpu_custom_call" | custom-call | tf_op jit(solution)/shard_map/pallas_call | solution.py:414
  50.8 0.6 %copy.17 = f32[2,512]{1,0:T(2,128)} copy(f32[2,512]{1,0:T(2,128)S(1)} %get-tuple-element.4) | data formatting | bytes 8192
  51.4 0.6 %copy.18 = f32[32,32]{1,0:T(8,128)} copy(f32[32,32]{1,0:T(8,128)S(1)} %get-tuple-element.5) | data formatting | bytes 8192

commit v4 on v3

--- a/solution.py
+++ b/solution.py
@@ -17,7 +17,7 @@
 QPAD = 384
 COORD_ROW, COORD_COL, PROJ_ROW, PROJ_COL, POT_COL, POT_ROW = range(6)
 DENS_PAIR, DENS_ROW, DENS_COL, DENS_OUT, DENS_SWAP = range(6, 11)
-ALPHA_PAIR, ALPHA_ROW, ALPHA_COL, ALPHA_SWAP = range(11, 15)
+ALPHA_ROW, ALPHA_COL = range(11, 13)
 
 
 def real_basis():
@@ -82,7 +82,7 @@
     p_out, p_in, q_out, q_in, z_out, z_in, y_out, y_in,
     k_out, k_in, h_out, h_in, c16,
     d_out, d_pair, d_sum, d_in, e_out, e_in, f_out, f_in,
-    a_out, a_pair, b_out, b_in, g_out, g_in, a_full,
+    a_out, a_in, b_out, b_in,
     arow, brow, t_all, tt_hi, tt_lo, lam, wt, z_wide, perm_f, perm_b, scr, m_hi, m_lo,
     send_sems, recv_sems, local_sems,
 ):
@@ -95,16 +95,17 @@
             return {"row": 2 * peer + core}
         return {group: peer}
 
-    def peers(group, body):
+    def nth_peer(group, i):
         size, me = groups[group]
         half = size // 2
-
+        return lax.rem(me + jnp.where(i < half, half + i, i - half + 1), size)
+
+    def peers(group, body):
         def step(i, carry):
-            ahead = jnp.where(i < half, half + i, i - half + 1)
-            body(lax.rem(me + ahead, size))
+            body(nth_peer(group, i))
             return carry
 
-        lax.fori_loop(0, size - 1, step, 0)
+        lax.fori_loop(0, groups[group][0] - 1, step, 0)
 
     def copy_to(device_id, which, source, target):
         return pltpu.make_async_remote_copy(
@@ -142,13 +143,20 @@
     sibling = {"row": r + 1 - 2 * core}
 
     barrier = pltpu.get_barrier_semaphore()
-    for axis in ("row", "col"):
-        peers(
-            axis,
-            lambda peer, axis=axis: pl.semaphore_signal(
-                barrier, inc=1, device_id={axis: peer}, device_id_type=MESH
-            ),
-        )
+
+    def hello(i, carry):
+        for axis in ("col", "row"):
+            peer = nth_peer(axis, i)
+            pl.semaphore_signal(barrier, inc=1, device_id={axis: peer}, device_id_type=MESH)
+        return carry
+
+    def hello_row(i, carry):
+        peer = nth_peer("row", i)
+        pl.semaphore_signal(barrier, inc=1, device_id={"row": peer}, device_id_type=MESH)
+        return carry
+
+    lax.fori_loop(0, NC - 1, hello, 0)
+    lax.fori_loop(NC - 1, NR - 1, hello_row, 0)
     near = pl.multiple_of((r // 8) * 128, 128)
     far = pl.multiple_of((r // 8) * 128 + 512, 128)
     fetches = [
@@ -210,8 +218,13 @@
     k_out[...] = k_row.astype(F32)
 
     pl.semaphore_wait(barrier, NR + NC - 2)
-    send("row", COORD_ROW, lambda peer: k_out, k_in)
-    send("row", PROJ_ROW, lambda peer: p_out.at[peer], p_in)
+
+    def first_sends(peer):
+        target = {"row": peer}
+        copy_to(target, PROJ_ROW, p_out.at[peer], p_in.at[r]).start()
+        copy_to(target, COORD_ROW, k_out, k_in.at[r]).start()
+
+    peers("row", first_sends)
     k_in[pl.ds(r, 1)] = k_out[...].reshape(1, 1, 128)
     p_in[pl.ds(r, 1)] = p_out[pl.ds(r, 1)]
 
@@ -239,6 +252,14 @@
     d_sum[...] = d_out[pl.ds(mine, NU)] + d_pair[...]
     send("chip", DENS_ROW, lambda peer: d_sum.at[peer], d_in)
     d_in[pl.ds(chip, 1)] = d_sum[pl.ds(chip, 1)]
+
+    energy = jnp.concatenate(
+        [jnp.broadcast_to(en_ref[k : k + 1, :], (16, 16)) for k in range(2)], axis=0
+    )
+    same = (iota((32, 16), 0) & 15) == iota((32, 16), 1)
+    e_col = jnp.sum(jnp.where(same, energy, 0.0), axis=1, keepdims=True)
+    ex128 = e_col * x128
+    alpha_energy = dot(x128, ex128, 0, 0, precision=HIGH)[:32]
 
     for fetch in fetches[8:]:
         fetch.wait()
@@ -324,30 +345,17 @@
     send("col", POT_COL, lambda peer: z_out.at[peer], z_in)
     z_in[pl.ds(c, 1)] = z_out[pl.ds(c, 1)]
 
-    energy = jnp.concatenate(
-        [jnp.broadcast_to(en_ref[k : k + 1, :], (16, 16)) for k in range(2)], axis=0
-    )
-    same = (iota((32, 16), 0) & 15) == iota((32, 16), 1)
-    e_col = jnp.sum(jnp.where(same, energy, 0.0), axis=1, keepdims=True)
-    ex128 = e_col * x128
-    alpha_energy = dot(x128, ex128, 0, 0, precision=HIGH)[:32]
     alpha_direct = dot(mode.astype(BF16), jnp.concatenate([high, high], axis=0), 1, 1)
     kept_g = jnp.where((row64 >> 5) == ((lane64 >> 5) & 1), alpha_direct, 0.0)
     part = alpha_energy - fold(kept_g[:32] + kept_g[32:], 32) * (1.0 / NK)
-    packed = dot(gather8, jnp.where(lane_is_t, part, 0.0), precision=HIGH)
-    a_out[0] = packed[0:4]
-    a_out[1] = packed[4:8]
-    copy_to(sibling, ALPHA_PAIR, a_out.at[1 - core], a_pair.at[0]).start()
+    a_out[...] = dot(gather8, jnp.where(lane_is_t, part, 0.0), precision=HIGH)
+    send("row", ALPHA_ROW, lambda peer: a_out, a_in)
+    a_in[pl.ds(r, 1)] = a_out[...].reshape(1, 8, 128)
 
     arrived("col", DENS_COL, e_in)
     f_out[...] = jnp.sum(e_in[...], axis=0)
     send("chip", DENS_OUT, lambda peer: f_out, f_in, base=mine)
     f_in[pl.ds(mine + chip, 1)] = f_out[...].reshape(1, 8, 128)
-
-    arrived_pair(ALPHA_PAIR, a_pair)
-    b_out[...] = a_out[pl.ds(core, 1)] + a_pair[...]
-    send("chip", ALPHA_ROW, lambda peer: b_out.at[0], b_in)
-    b_in[pl.ds(chip, 1)] = b_out[...]
 
     c8[...] = jnp.zeros((8, 256), F32)
     for j in range(4):
@@ -361,10 +369,10 @@
     send("row", POT_ROW, lambda peer: y_out.at[peer], y_in)
     y_in[pl.ds(r, 1)] = y_out[pl.ds(r, 1)]
 
-    arrived("chip", ALPHA_ROW, b_in)
-    g_out[...] = jnp.sum(b_in[...], axis=0, keepdims=True)
-    send("col", ALPHA_COL, lambda peer: g_out.at[0], g_in)
-    g_in[pl.ds(c, 1)] = g_out[...]
+    arrived("row", ALPHA_ROW, a_in)
+    b_out[...] = jnp.sum(a_in[...], axis=0)
+    send("col", ALPHA_COL, lambda peer: b_out, b_in)
+    b_in[pl.ds(c, 1)] = b_out[...].reshape(1, 8, 128)
 
     arrived("chip", DENS_OUT, f_in)
     half = f_in.at[pl.ds(mine, NU)]
@@ -382,12 +390,8 @@
     exchange = total_of(dot(quarters, w_hi) + dot(quarters, w_lo))
     alpha_exchange = total_of(dot(density, weighted, 0, 0, precision=HIGH))
 
-    arrived("col", ALPHA_COL, g_in)
-    a_full[pl.ds(core, 1)] = jnp.sum(g_in[...], axis=0, keepdims=True)
-    copy_to(sibling, ALPHA_SWAP, a_full.at[core], a_full.at[core]).start()
-    arrived_pair(ALPHA_SWAP, a_full.at[1 - core])
-    shares = dot(spread[:, 0:4], a_full[0], precision=HIGH)
-    shares = shares + dot(spread[:, 4:8], a_full[1], precision=HIGH)
+    arrived("col", ALPHA_COL, b_in)
+    shares = dot(spread, jnp.sum(b_in[...], axis=0), precision=HIGH)
     shares = fold(jnp.where(lane_is_t, shares, 0.0), 64, 32)
     alpha = (shares + (2.0 / NT) * alpha_exchange) * (1.0 / NT)
     alpha_ref[...] = alpha[:, :32]
@@ -457,13 +461,10 @@
             pltpu.VMEM((NC, 8, 128), F32),
             pltpu.VMEM((8, 128), F32),
             pltpu.VMEM((NR, 8, 128), F32),
-            pltpu.VMEM((2, 4, 128), F32),
-            pltpu.VMEM((1, 4, 128), F32),
-            pltpu.VMEM((1, 4, 128), F32),
-            pltpu.VMEM((NU, 4, 128), F32),
-            pltpu.VMEM((1, 4, 128), F32),
-            pltpu.VMEM((NC, 4, 128), F32),
-            pltpu.VMEM((2, 4, 128), F32),
+            pltpu.VMEM((8, 128), F32),
+            pltpu.VMEM((NR, 8, 128), F32),
+            pltpu.VMEM((8, 128), F32),
+            pltpu.VMEM((NC, 8, 128), F32),
             pltpu.VMEM((2, 32, 512), F32),
             pltpu.VMEM((2, 32, 512), F32),
             pltpu.VMEM((2048, NK), BF16),
@@ -477,8 +478,8 @@
             pltpu.VMEM((2, QPAD, 128), F32),
             pltpu.VMEM((QPAD, NK), BF16),
             pltpu.VMEM((QPAD, NK), BF16),
-            pltpu.SemaphoreType.DMA((15,)),
-            pltpu.SemaphoreType.DMA((15,)),
+            pltpu.SemaphoreType.DMA((13,)),
+            pltpu.SemaphoreType.DMA((13,)),
             pltpu.SemaphoreType.DMA((14,)),
         ],
         compiler_params=pltpu.CompilerParams(

time: 52.1 us -> 50.1 us (0.962); the launches traced: 52 us -> 49.3 us
  Pallas kernels: 50.1 us -> 47.5 us
    pallas_call x1, Pallas kernels: 50.1 us -> 47.5 us  [on_device(): pl.pallas_call(kernel, out_shape=(jax.ShapeDtypeStruct((2, 512), F32), ja...]
where the time goes in v4:
time: 50.1 us; the launch traced here: 49.3 us
  Pallas kernels  47.5 us (95%)
  local copies, waits for them, and re-layouts  1.2 us (2%)
  between operations  0.64 us (1%)
    pallas_call x1, Pallas kernels, on_device(): pl.pallas_call(kernel, out_shape=(jax.ShapeDtypeStruct((2, 512), F32), ja...  47.5 us
    unnamed x2, local copies, waits for them, and re-layouts  1.2 us

profile of v4, /device:TPU:1, one launch (start us, length us, event | category | flops | bytes accessed | tf_op | source)
XLA Modules:
  0.0 49.3 jit_solution(679179748554021939)
XLA Ops:
  0.6 47.5 %shard_map.140 = (f32[2,512]{1,0:T(2,128)S(1)}, f32[32,32]{1,0:T(8,128)S(1)}) custom-call(bf16[2,16,1024]{2,1,0:T(8,128)(2,1)} %pe_hbm.1, bf16[2,4,1024]{2,1,0:T(4,128)(2,1)} %cond_hbm.1, bf16[2,4,1024]{2,1,0:T(4,128)(2,1)} %val_hbm.1, f32[1,1024]{1,0:T(1,128)} %bitcast.1, f32[2,16]{1,0:T(2,128)} %en_hbm.1, bf16[2,512]{1,0:T(2,128)(2,1)} %vec_hbm.1, ...), custom_call_target="tpu_custom_call" | custom-call | tf_op jit(solution)/shard_map/pallas_call | solution.py:418
  48.1 0.6 %copy.17 = f32[2,512]{1,0:T(2,128)} copy(f32[2,512]{1,0:T(2,128)S(1)} %get-tuple-element.4) | data formatting | bytes 8192
  48.7 0.6 %copy.18 = f32[32,32]{1,0:T(8,128)} copy(f32[32,32]{1,0:T(8,128)S(1)} %get-tuple-element.5) | data formatting | bytes 8192

commit v5 on v4

--- a/solution.py
+++ b/solution.py
@@ -218,13 +218,8 @@
     k_out[...] = k_row.astype(F32)
 
     pl.semaphore_wait(barrier, NR + NC - 2)
-
-    def first_sends(peer):
-        target = {"row": peer}
-        copy_to(target, PROJ_ROW, p_out.at[peer], p_in.at[r]).start()
-        copy_to(target, COORD_ROW, k_out, k_in.at[r]).start()
-
-    peers("row", first_sends)
+    send("row", COORD_ROW, lambda peer: k_out, k_in)
+    send("row", PROJ_ROW, lambda peer: p_out.at[peer], p_in)
     k_in[pl.ds(r, 1)] = k_out[...].reshape(1, 1, 128)
     p_in[pl.ds(r, 1)] = p_out[pl.ds(r, 1)]
 
@@ -348,7 +343,8 @@
     alpha_direct = dot(mode.astype(BF16), jnp.concatenate([high, high], axis=0), 1, 1)
     kept_g = jnp.where((row64 >> 5) == ((lane64 >> 5) & 1), alpha_direct, 0.0)
     part = alpha_energy - fold(kept_g[:32] + kept_g[32:], 32) * (1.0 / NK)
-    a_out[...] = dot(gather8, jnp.where(lane_is_t, part, 0.0), precision=HIGH)
+    packed = dot(gather8, jnp.where(lane_is_t, part, 0.0), precision=HIGH)
+    a_out[...] = packed.astype(BF16)
     send("row", ALPHA_ROW, lambda peer: a_out, a_in)
     a_in[pl.ds(r, 1)] = a_out[...].reshape(1, 8, 128)
 
@@ -370,7 +366,7 @@
     y_in[pl.ds(r, 1)] = y_out[pl.ds(r, 1)]
 
     arrived("row", ALPHA_ROW, a_in)
-    b_out[...] = jnp.sum(a_in[...], axis=0)
+    b_out[...] = jnp.sum(a_in[...].astype(F32), axis=0)
     send("col", ALPHA_COL, lambda peer: b_out, b_in)
     b_in[pl.ds(c, 1)] = b_out[...].reshape(1, 8, 128)
 
@@ -388,21 +384,35 @@
         return fold(v[0:32] + v[32:64] + v[64:96] + v[96:128], 64, 32)
 
     exchange = total_of(dot(quarters, w_hi) + dot(quarters, w_lo))
-    alpha_exchange = total_of(dot(density, weighted, 0, 0, precision=HIGH))
+    alpha_exchange = total_of(dot(density, weighted, 0, 0, precision=HIGH)) * (2.0 / NT / NT)
+    x32 = x128[:, :32]
+    base = ex128 + (2.0 / NT) * exchange - dot(x32, alpha_exchange, precision=HIGH)
+    base = jnp.where(lane_is_t, base, 0.0)
+    pick_m = iota((32, 8), 0)
+    x_by_u = jnp.concatenate(
+        [dot(x32, one_hot(pick_m == 4 * iota((32, 8), 1) + u), precision=HIGH) for u in range(4)],
+        axis=0,
+    )
+
+    def four_blocks(v):
+        v = jnp.where(own128, v, 0.0)
+        return v[0:32] + v[32:64] + v[64:96] + v[96:128]
 
     arrived("col", ALPHA_COL, b_in)
-    shares = dot(spread, jnp.sum(b_in[...], axis=0), precision=HIGH)
-    shares = fold(jnp.where(lane_is_t, shares, 0.0), 64, 32)
-    alpha = (shares + (2.0 / NT) * alpha_exchange) * (1.0 / NT)
-    alpha_ref[...] = alpha[:, :32]
-    base = ex128 + (2.0 / NT) * exchange - dot(x128[:, :32], alpha, precision=HIGH)
+    shares = jnp.sum(b_in[...], axis=0) * (1.0 / NT)
+    projected = four_blocks(dot(x_by_u, shares, precision=HIGH))
 
     arrived("row", POT_ROW, y_in)
     direct = jnp.where(own64, dot(lk[...], y_in[...].reshape(512, 128)), 0.0)
-    residual = base - fold(direct[:32] + direct[32:], 64, 32) * (1.0 / NK)
-    rows = dot(gather8, jnp.where(lane_is_t, residual, 0.0), precision=HIGH)
+    both = fold(projected + (direct[:32] + direct[32:]) * (1.0 / NK), 64, 32)
+    rows = base - jnp.where(lane_is_t, both, 0.0)
+    rows = rows + pltpu.roll(rows, 31, 0)
+    rows = rows + pltpu.roll(rows, 30, 0)
     for i in range(8):
-        out_ref[i // 4 : i // 4 + 1, (i % 4) * 128 : (i % 4 + 1) * 128] = rows[i : i + 1, :]
+        at = 128 * (i % 4)
+        out_ref[i // 4 : i // 4 + 1, at : at + 128] = rows[4 * i : 4 * i + 1, :]
+    alpha = fold(jnp.where(lane_is_t, dot(spread, shares, precision=HIGH), 0.0), 64, 32)
+    alpha_ref[...] = (alpha + alpha_exchange)[:, :32]
 
     for which, many in waits:
         wait_bytes(send_sems.at[which], many)
@@ -461,8 +471,8 @@
             pltpu.VMEM((NC, 8, 128), F32),
             pltpu.VMEM((8, 128), F32),
             pltpu.VMEM((NR, 8, 128), F32),
-            pltpu.VMEM((8, 128), F32),
-            pltpu.VMEM((NR, 8, 128), F32),
+            pltpu.VMEM((8, 128), BF16),
+            pltpu.VMEM((NR, 8, 128), BF16),
             pltpu.VMEM((8, 128), F32),
             pltpu.VMEM((NC, 8, 128), F32),
             pltpu.VMEM((2, 32, 512), F32),

time: 50.1 us -> 49.2 us (0.982)
  Pallas kernels: 47.5 us -> 46.6 us
    pallas_call x1, Pallas kernels: 47.5 us -> 46.6 us  [on_device(): pl.pallas_call(kernel, out_shape=(jax.ShapeDtypeStruct((2, 512), F32), ja...]
where the time goes in v5:
time: 49.2 us; the launch traced here: 48.4 us
  Pallas kernels  46.6 us (95%)
  local copies, waits for them, and re-layouts  1.2 us (2%)
  between operations  0.64 us (1%)
    pallas_call x1, Pallas kernels, on_device(): pl.pallas_call(kernel, out_shape=(jax.ShapeDtypeStruct((2, 512), F32), ja...  46.6 us
    unnamed x2, local copies, waits for them, and re-layouts  1.2 us

profile of v5, /device:TPU:1, one launch (start us, length us, event | category | flops | bytes accessed | tf_op | source)
XLA Modules:
  0.0 48.4 jit_solution(6452840321239329899)
XLA Ops:
  0.6 46.6 %shard_map.140 = (f32[2,512]{1,0:T(2,128)S(1)}, f32[32,32]{1,0:T(8,128)S(1)}) custom-call(bf16[2,16,1024]{2,1,0:T(8,128)(2,1)} %pe_hbm.1, bf16[2,4,1024]{2,1,0:T(4,128)(2,1)} %cond_hbm.1, bf16[2,4,1024]{2,1,0:T(4,128)(2,1)} %val_hbm.1, f32[1,1024]{1,0:T(1,128)} %bitcast.1, f32[2,16]{1,0:T(2,128)} %en_hbm.1, bf16[2,512]{1,0:T(2,128)(2,1)} %vec_hbm.1, ...), custom_call_target="tpu_custom_call" | custom-call | tf_op jit(solution)/shard_map/pallas_call | solution.py:428
  47.2 0.6 %copy.17 = f32[2,512]{1,0:T(2,128)} copy(f32[2,512]{1,0:T(2,128)S(1)} %get-tuple-element.4) | data formatting | bytes 8192
  47.8 0.6 %copy.18 = f32[32,32]{1,0:T(8,128)} copy(f32[32,32]{1,0:T(8,128)S(1)} %get-tuple-element.5) | data formatting | bytes 8192

commit v6 on v5

--- a/solution.py
+++ b/solution.py
@@ -96,9 +96,19 @@
         return {group: peer}
 
     def nth_peer(group, i):
-        size, me = groups[group]
-        half = size // 2
-        return lax.rem(me + jnp.where(i < half, half + i, i - half + 1), size)
+        me = groups[group][1]
+        if group == "col":
+            ways = jnp.where(lax.rem(i, 2) == 0, 1, 3)
+            y_step = jnp.where(i < 4, 2, jnp.where(i >= 12, 0, ways))
+            at = jnp.where((i >= 4) & (i < 12), (i - 4) // 2, lax.rem(i, 4))
+            x_step = jnp.where(at == 3, 0, jnp.where(at == 2, 3, 2 - at))
+            return lax.rem(me // 4 + x_step, 4) * 4 + lax.rem(lax.rem(me, 4) + y_step, 4)
+        inner = groups[group][0] // 8
+        at = i // inner
+        z_step = jnp.where(lax.rem(at, 2) == 1, 4 - (at + 1) // 2, 4 + at // 2)
+        z_step = jnp.where(at == 7, 0, z_step)
+        near = lax.rem(lax.rem(me, inner) + lax.rem(i, inner) + 1, inner)
+        return lax.rem(me // inner + z_step, 8) * inner + near
 
     def peers(group, body):
         def step(i, carry):
@@ -332,6 +342,12 @@
     high, low = split(scaled)
     wt[0:64, :] = high
     wt[64:128, :] = low
+    alpha_direct = dot(mode.astype(BF16), jnp.concatenate([high, high], axis=0), 1, 1)
+    kept_g = jnp.where((row64 >> 5) == ((lane64 >> 5) & 1), alpha_direct, 0.0)
+    part = alpha_energy - fold(kept_g[:32] + kept_g[32:], 32) * (1.0 / NK)
+    packed = dot(gather8, jnp.where(lane_is_t, part, 0.0), precision=HIGH)
+    a_out[...] = packed.astype(BF16)
+
     for k in range(2):
         both = dot(wt[...], tt_hi[k])
         back = both[:64] + both[64:] + dot(wt[0:64, :], tt_lo[k])
@@ -340,11 +356,6 @@
     send("col", POT_COL, lambda peer: z_out.at[peer], z_in)
     z_in[pl.ds(c, 1)] = z_out[pl.ds(c, 1)]
 
-    alpha_direct = dot(mode.astype(BF16), jnp.concatenate([high, high], axis=0), 1, 1)
-    kept_g = jnp.where((row64 >> 5) == ((lane64 >> 5) & 1), alpha_direct, 0.0)
-    part = alpha_energy - fold(kept_g[:32] + kept_g[32:], 32) * (1.0 / NK)
-    packed = dot(gather8, jnp.where(lane_is_t, part, 0.0), precision=HIGH)
-    a_out[...] = packed.astype(BF16)
     send("row", ALPHA_ROW, lambda peer: a_out, a_in)
     a_in[pl.ds(r, 1)] = a_out[...].reshape(1, 8, 128)
 

time: 49.2 us -> 47.7 us (0.970)
  Pallas kernels: 46.6 us -> 45.1 us
    pallas_call x1, Pallas kernels: 46.6 us -> 45.1 us  [on_device(): pl.pallas_call(kernel, out_shape=(jax.ShapeDtypeStruct((2, 512), F32), ja...]
where the time goes in v6:
time: 47.7 us; the launch traced here: 46.9 us
  Pallas kernels  45.1 us (95%)
  local copies, waits for them, and re-layouts  1.2 us (3%)
  between operations  0.64 us (1%)
    pallas_call x1, Pallas kernels, on_device(): pl.pallas_call(kernel, out_shape=(jax.ShapeDtypeStruct((2, 512), F32), ja...  45.1 us
    unnamed x2, local copies, waits for them, and re-layouts  1.2 us

profile of v6, /device:TPU:1, one launch (start us, length us, event | category | flops | bytes accessed | tf_op | source)
XLA Modules:
  0.0 46.9 jit_solution(1589804040211502065)
XLA Ops:
  0.6 45.1 %shard_map.140 = (f32[2,512]{1,0:T(2,128)S(1)}, f32[32,32]{1,0:T(8,128)S(1)}) custom-call(bf16[2,16,1024]{2,1,0:T(8,128)(2,1)} %pe_hbm.1, bf16[2,4,1024]{2,1,0:T(4,128)(2,1)} %cond_hbm.1, bf16[2,4,1024]{2,1,0:T(4,128)(2,1)} %val_hbm.1, f32[1,1024]{1,0:T(1,128)} %bitcast.1, f32[2,16]{1,0:T(2,128)} %en_hbm.1, bf16[2,512]{1,0:T(2,128)(2,1)} %vec_hbm.1, ...), custom_call_target="tpu_custom_call" | custom-call | tf_op jit(solution)/shard_map/pallas_call | solution.py:439
  45.7 0.6 %copy.17 = f32[2,512]{1,0:T(2,128)} copy(f32[2,512]{1,0:T(2,128)S(1)} %get-tuple-element.4) | data formatting | bytes 8192
  46.3 0.6 %copy.18 = f32[32,32]{1,0:T(8,128)} copy(f32[32,32]{1,0:T(8,128)S(1)} %get-tuple-element.5) | data formatting | bytes 8192

commit v7 on v6

--- a/solution.py
+++ b/solution.py
@@ -95,27 +95,24 @@
             return {"row": 2 * peer + core}
         return {group: peer}
 
-    def nth_peer(group, i):
-        me = groups[group][1]
-        if group == "col":
-            ways = jnp.where(lax.rem(i, 2) == 0, 1, 3)
-            y_step = jnp.where(i < 4, 2, jnp.where(i >= 12, 0, ways))
-            at = jnp.where((i >= 4) & (i < 12), (i - 4) // 2, lax.rem(i, 4))
-            x_step = jnp.where(at == 3, 0, jnp.where(at == 2, 3, 2 - at))
-            return lax.rem(me // 4 + x_step, 4) * 4 + lax.rem(lax.rem(me, 4) + y_step, 4)
-        inner = groups[group][0] // 8
-        at = i // inner
-        z_step = jnp.where(lax.rem(at, 2) == 1, 4 - (at + 1) // 2, 4 + at // 2)
-        z_step = jnp.where(at == 7, 0, z_step)
-        near = lax.rem(lax.rem(me, inner) + lax.rem(i, inner) + 1, inner)
-        return lax.rem(me // inner + z_step, 8) * inner + near
+    z_at = [lax.rem(r // 4 + step, 8) for step in range(8)]
+    near_at = [lax.rem(lax.rem(r, 4) + step, 4) for step in range(4)]
+    y_lo_at = lax.rem(r, 4) // 2
+    x_at = [lax.rem(c // 4 + step, 4) * 4 for step in range(4)]
+    y_at = [lax.rem(lax.rem(c, 4) + step, 4) for step in range(4)]
+    z_order = (4, 3, 5, 2, 6, 1, 7, 0)
+    x_order = (2, 1, 3, 0)
+    partners = {
+        "row": [z_at[z] * 4 + near_at[n] for z in z_order for n in (1, 2, 3, 0)][:-1],
+        "chip": [z_at[z] * 2 + y for z in z_order for y in (1 - y_lo_at, y_lo_at)][:-1],
+        "col": [x_at[x] + y_at[2] for x in x_order]
+        + [x_at[x] + y_at[y] for x in x_order for y in (1, 3)]
+        + [x_at[x] + y_at[0] for x in x_order][:-1],
+    }
 
     def peers(group, body):
-        def step(i, carry):
-            body(nth_peer(group, i))
-            return carry
-
-        lax.fori_loop(0, groups[group][0] - 1, step, 0)
+        for peer in partners[group]:
+            body(peer)
 
     def copy_to(device_id, which, source, target):
         return pltpu.make_async_remote_copy(
@@ -153,20 +150,11 @@
     sibling = {"row": r + 1 - 2 * core}
 
     barrier = pltpu.get_barrier_semaphore()
-
-    def hello(i, carry):
+    for i in range(NR - 1):
         for axis in ("col", "row"):
-            peer = nth_peer(axis, i)
-            pl.semaphore_signal(barrier, inc=1, device_id={axis: peer}, device_id_type=MESH)
-        return carry
-
-    def hello_row(i, carry):
-        peer = nth_peer("row", i)
-        pl.semaphore_signal(barrier, inc=1, device_id={"row": peer}, device_id_type=MESH)
-        return carry
-
-    lax.fori_loop(0, NC - 1, hello, 0)
-    lax.fori_loop(NC - 1, NR - 1, hello_row, 0)
+            if i < groups[axis][0] - 1:
+                there = {axis: partners[axis][i]}
+                pl.semaphore_signal(barrier, inc=1, device_id=there, device_id_type=MESH)
     near = pl.multiple_of((r // 8) * 128, 128)
     far = pl.multiple_of((r // 8) * 128 + 512, 128)
     fetches = [

time: 47.7 us -> 47.5 us (level)
  no operation moved by 1% of the time
where the time goes in v7:
time: 47.5 us; the launch traced here: 46.6 us
  Pallas kernels  44.7 us (94%)
  local copies, waits for them, and re-layouts  1.2 us (3%)
  between operations  0.64 us (1%)
    pallas_call x1, Pallas kernels, on_device(): pl.pallas_call(kernel, out_shape=(jax.ShapeDtypeStruct((2, 512), F32), ja...  44.7 us
    unnamed x2, local copies, waits for them, and re-layouts  1.2 us

profile of v7, /device:TPU:1, one launch (start us, length us, event | category | flops | bytes accessed | tf_op | source)
XLA Modules:
  0.0 46.6 jit_solution(10397801814275643324)
XLA Ops:
  0.6 44.7 %shard_map.140 = (f32[2,512]{1,0:T(2,128)S(1)}, f32[32,32]{1,0:T(8,128)S(1)}) custom-call(bf16[2,16,1024]{2,1,0:T(8,128)(2,1)} %pe_hbm.1, bf16[2,4,1024]{2,1,0:T(4,128)(2,1)} %cond_hbm.1, bf16[2,4,1024]{2,1,0:T(4,128)(2,1)} %val_hbm.1, f32[1,1024]{1,0:T(1,128)} %bitcast.1, f32[2,16]{1,0:T(2,128)} %en_hbm.1, bf16[2,512]{1,0:T(2,128)(2,1)} %vec_hbm.1, ...), custom_call_target="tpu_custom_call" | custom-call | tf_op jit(solution)/shard_map/pallas_call | solution.py:427
  45.4 0.6 %copy.17 = f32[2,512]{1,0:T(2,128)} copy(f32[2,512]{1,0:T(2,128)S(1)} %get-tuple-element.4) | data formatting | bytes 8192
  45.9 0.6 %copy.18 = f32[32,32]{1,0:T(8,128)} copy(f32[32,32]{1,0:T(8,128)S(1)} %get-tuple-element.5) | data formatting | bytes 8192

commit v8 on v7

--- a/solution.py
+++ b/solution.py
@@ -15,6 +15,7 @@
 NK, NT = 1024, 16384
 NQ = 289
 QPAD = 384
+EARLY = 16
 COORD_ROW, COORD_COL, PROJ_ROW, PROJ_COL, POT_COL, POT_ROW = range(6)
 DENS_PAIR, DENS_ROW, DENS_COL, DENS_OUT, DENS_SWAP = range(6, 11)
 ALPHA_ROW, ALPHA_COL = range(11, 13)
@@ -83,7 +84,7 @@
     k_out, k_in, h_out, h_in, c16,
     d_out, d_pair, d_sum, d_in, e_out, e_in, f_out, f_in,
     a_out, a_in, b_out, b_in,
-    arow, brow, t_all, tt_hi, tt_lo, lam, wt, z_wide, perm_f, perm_b, scr, m_hi, m_lo,
+    arow, brow, t_all, tt_hi, tt_lo, lam, modes, wt, z_wide, perm_f, perm_b, scr, m_hi, m_lo,
     send_sems, recv_sems, local_sems,
 ):
     r, c = lax.axis_index("row"), lax.axis_index("col")
@@ -307,34 +308,34 @@
         for i in range(4):
             at = 128 * i
             outer = dot(first[:, at : at + 128], qa_ref[...], 0, 0)
-            inner = dot(second[:, at : at + 128], qb_ref[...], 0, 0)
-            high, low = split(outer * inner)
-            t_all[512 * k + at : 512 * k + at + 128, :] = high
-            t_all[1024 + 512 * k + at : 1024 + 512 * k + at + 128, :] = low
-
-    def build_basis(j, carry):
-        at = pl.multiple_of(j * 32, 32)
-        for k in range(2):
-            high, low = split(arow[k, pl.ds(j, 1), :] * brow[k])
-            tt_hi[k, pl.ds(at, 32), :] = high
-            tt_lo[k, pl.ds(at, 32), :] = low
-        return carry
-
-    lax.fori_loop(0, 32, build_basis, 0)
+            inner = dot(second[:, at : at + 128], qb_ref[:, :128], 0, 0)
+            for b in range(8):
+                high, low = split(outer[:, 128 * b : 128 * b + 128] * inner)
+                lanes = slice(128 * b, 128 * b + 128)
+                t_all[512 * k + at : 512 * k + at + 128, lanes] = high
+                t_all[1024 + 512 * k + at : 1024 + 512 * k + at + 128, lanes] = low
+
+    def turn_basis(outer_modes):
+        for j in outer_modes:
+            for k in range(2):
+                high, low = split(arow[k, j : j + 1, :] * brow[k])
+                tt_hi[k, 32 * j : 32 * j + 32, :] = high
+                tt_lo[k, 32 * j : 32 * j + 32, :] = low
+
+    turn_basis(range(EARLY))
 
     arrived("col", PROJ_COL, q_in)
     turned = jnp.transpose(q_in[...].reshape(512, 128).astype(F32)).astype(BF16)
-    mode = dot(jnp.concatenate([turned[:64], turned[64:]] * 2, axis=1), t_all[...])
-    first_g = iota((64, NK), 0) < 32
-    scaled = jnp.where(first_g, lam[0:1, :], lam[1:2, :]) * mode
-    high, low = split(scaled)
-    wt[0:64, :] = high
-    wt[64:128, :] = low
-    alpha_direct = dot(mode.astype(BF16), jnp.concatenate([high, high], axis=0), 1, 1)
-    kept_g = jnp.where((row64 >> 5) == ((lane64 >> 5) & 1), alpha_direct, 0.0)
-    part = alpha_energy - fold(kept_g[:32] + kept_g[32:], 32) * (1.0 / NK)
-    packed = dot(gather8, jnp.where(lane_is_t, part, 0.0), precision=HIGH)
-    a_out[...] = packed.astype(BF16)
+    turned = jnp.concatenate([turned[:64], turned[64:]] * 2, axis=1)
+    first_g = iota((64, 256), 0) < 32
+    for i in range(4):
+        lanes = slice(256 * i, 256 * i + 256)
+        mode = dot(turned, t_all[:, lanes])
+        turn_basis(range(EARLY + (32 - EARLY) // 4 * i, EARLY + (32 - EARLY) // 4 * (i + 1)))
+        high, low = split(jnp.where(first_g, lam[0:1, lanes], lam[1:2, lanes]) * mode)
+        modes[:, lanes] = mode.astype(BF16)
+        wt[0:64, lanes] = high
+        wt[64:128, lanes] = low
 
     for k in range(2):
         both = dot(wt[...], tt_hi[k])
@@ -344,6 +345,12 @@
     send("col", POT_COL, lambda peer: z_out.at[peer], z_in)
     z_in[pl.ds(c, 1)] = z_out[pl.ds(c, 1)]
 
+    high = wt[0:64, :]
+    alpha_direct = dot(modes[...], jnp.concatenate([high, high], axis=0), 1, 1)
+    kept_g = jnp.where((row64 >> 5) == ((lane64 >> 5) & 1), alpha_direct, 0.0)
+    part = alpha_energy - fold(kept_g[:32] + kept_g[32:], 32) * (1.0 / NK)
+    part = jnp.where(lane_is_t, part, 0.0).astype(BF16)
+    a_out[...] = dot(gather8.astype(BF16), part).astype(BF16)
     send("row", ALPHA_ROW, lambda peer: a_out, a_in)
     a_in[pl.ds(r, 1)] = a_out[...].reshape(1, 8, 128)
 
@@ -480,6 +487,7 @@
             pltpu.VMEM((2, NK, 512), BF16),
             pltpu.VMEM((2, NK, 512), BF16),
             pltpu.VMEM((8, NK), F32),
+            pltpu.VMEM((64, NK), BF16),
             pltpu.VMEM((128, NK), BF16),
             pltpu.VMEM((128, 512), F32),
             pltpu.VMEM((512, 512), BF16),

time: 47.5 us -> 47.5 us (level)
  the two profiles are of different devices: /device:TPU:1 before, /device:TPU:8 now
where the time goes in v8:
time: 47.5 us; the launch traced here: 47.4 us
  Pallas kernels  45.5 us (96%)
  local copies, waits for them, and re-layouts  1.2 us (3%)
  between operations  0.64 us (1%)
    pallas_call x1, Pallas kernels, on_device(): pl.pallas_call(kernel, out_shape=(jax.ShapeDtypeStruct((2, 512), F32), ja...  45.5 us
    unnamed x2, local copies, waits for them, and re-layouts  1.2 us

profile of v8, /device:TPU:8, one launch (start us, length us, event | category | flops | bytes accessed | tf_op | source)
XLA Modules:
  0.0 47.4 jit_solution(4821142045337443701)
XLA Ops:
  0.6 45.5 %shard_map.140 = (f32[2,512]{1,0:T(2,128)S(1)}, f32[32,32]{1,0:T(8,128)S(1)}) custom-call(bf16[2,16,1024]{2,1,0:T(8,128)(2,1)} %pe_hbm.1, bf16[2,4,1024]{2,1,0:T(4,128)(2,1)} %cond_hbm.1, bf16[2,4,1024]{2,1,0:T(4,128)(2,1)} %val_hbm.1, f32[1,1024]{1,0:T(1,128)} %bitcast.1, f32[2,16]{1,0:T(2,128)} %en_hbm.1, bf16[2,512]{1,0:T(2,128)(2,1)} %vec_hbm.1, ...), custom_call_target="tpu_custom_call" | custom-call | tf_op jit(solution)/shard_map/pallas_call | solution.py:434
  46.2 0.6 %copy.17 = f32[2,512]{1,0:T(2,128)} copy(f32[2,512]{1,0:T(2,128)S(1)} %get-tuple-element.4) | data formatting | bytes 8192
  46.8 0.6 %copy.18 = f32[32,32]{1,0:T(8,128)} copy(f32[32,32]{1,0:T(8,128)S(1)} %get-tuple-element.5) | data formatting | bytes 8192
